TPU v7x, 128 devices: a whole 4x4x4 slice. The times are simulated.
128 devices in a mesh: owner: 128 (over z, y, x, core).
Axes of the slice: x: 4, y: 4, z: 4, core: 2. Of those that a mesh axis runs over, the one named last changes fastest.
Arguments:
- frontier: bfloat16 [2048, 1326], P('owner'), may hold values from 0.019897461 to 1
- policy_table: bfloat16 [2048, 1326], replicated, may hold values from 0.019897461 to 1
- first_counts: int32 [2048], P('owner'), may hold values from 1 to 64
- policy_index: int32 [3, 65536], P(None, 'owner'), may hold values from 0 to 2047
- owner_index: int32 [3, 65536], P(None, 'owner'), may hold values from 0 to 127
- next_counts: int32 [2, 65536], P(None, 'owner'), may hold values from 0 to 64, as said below
- value_in: bfloat16 [1326, 1536], replicated, may hold values from -0.15625 to 0.15625
- value_out: bfloat16 [1536, 1326], replicated, may hold values from -0.15625 to 0.15625
Outputs:
- leaf_values: bfloat16 [3, 65536, 1326], P(None, 'owner')
Inputs may be any that keep to these rules, and one draw needn't show every extreme that they name: `next_counts`: 0 marks a belief that is not expanded.
All inputs are finite; a program needn't handle non-finite values.
Results may differ from a plain program's by a relative error of at most 0.0067.
Values may be sent and summed in bfloat16 or wider, within the bound.
No kernel may reach another device: no remote copies, remote signals or barrier semaphores. Data moves between devices by JAX's collectives and lax.ppermute only.
A program may use at most 128 MiB of HBM per device.

v0:
```python
import jax
import jax.numpy as jnp
from jax import lax
from jax.experimental import pallas as pl
from jax.experimental.pallas import tpu as pltpu
from jax.sharding import Mesh
from jax.sharding import PartitionSpec as P

HANDS = 1326
HIDDEN = 1536
POLICY = 2048
SLOTS = 512
DEVICES = 128
CHIPS = 64
FRONT = 16
CAP = 4
KEPT = 384 * DEVICES
CHUNKS = 11
WIDTH = CHUNKS * 128
FROWS = FRONT * CHUNKS
COMMON = 38
TROWS = COMMON + 2
BROWS = FROWS + TROWS
STRIDE = 16
BLOCK = 256
OWNER = ("owner_0", "owner_1", "owner_2", "owner_3")
F32 = jnp.float32
BF16 = jnp.bfloat16
I32 = jnp.int32


def iota(shape, dim):
    return lax.broadcasted_iota(I32, shape, dim)


def mm(a, b, dims):
    return lax.dot_general(a.astype(BF16), b.astype(BF16), (dims, ((), ())), preferred_element_type=F32)


NN = ((1,), (0,))
NT = ((1,), (1,))
TN = ((0,), (0,))


def tables_kernel(first_ref, owner_ref, policy_ref, next_ref, common_ref, spec_ref):
    lane = iota((1, SLOTS), 1)
    segment = jnp.zeros((1, SLOTS), I32)
    running = jnp.int32(0)
    for k in range(FRONT):
        running = running + first_ref[k]
        if k < FRONT - 1:
            segment = segment + (running <= lane).astype(I32)
    total = jnp.minimum(running, SLOTS)
    upper = (iota((SLOTS, SLOTS), 0) <= iota((SLOTS, SLOTS), 1)).astype(F32).astype(BF16)
    rows = []
    for level in range(3):
        hit = iota((DEVICES, SLOTS), 0) == owner_ref[level : level + 1, :]
        rank = mm(hit.astype(F32), upper, NN)
        policy = policy_ref[level : level + 1, :]
        fields = [lane - SLOTS // 2, jnp.ones_like(lane), lax.shift_right_logical(policy, 4), policy & 15]
        fields.append(next_ref[level : level + 1, :] if level < 2 else jnp.zeros_like(lane))
        fields.append(segment)
        values = jnp.concatenate(fields + [jnp.zeros_like(lane)] * 2, axis=0).astype(F32)
        found = []
        for r in range(CAP):
            mask = jnp.where(hit & (rank == r + 1), 1.0, 0.0)
            found.append(mm(values, mask, NT))
        slot = [f[0:1] + (SLOTS // 2) * (1.0 - f[1:2]) for f in found]
        high = [f[2:3] for f in found]
        low = [f[3:4] for f in found]
        count = [f[4:5] for f in found]
        parent = [f[5:6] for f in found]
        if level == 0:
            rows += slot + count + high + low + parent
        elif level == 1:
            rows += slot + count + high + low
        else:
            last = slot + high + low
    lanes = jnp.zeros((1, DEVICES), F32)
    zero = [lanes]
    common = rows + [lanes + (total - SLOTS // 2).astype(F32)] + zero
    common = jnp.concatenate(common + zero * (40 - len(common)), axis=0)
    common_ref[...] = common.astype(BF16)
    spec = jnp.concatenate(rows + last + zero * (DEVICES - len(rows) - len(last)), axis=0)
    spec_ref[...] = jnp.transpose(spec).astype(BF16)


def tables(first, owner, policy, following):
    vm = pl.BlockSpec(memory_space=pltpu.VMEM)
    return pl.pallas_call(
        tables_kernel,
        out_shape=[
            jax.ShapeDtypeStruct((40, DEVICES), BF16),
            jax.ShapeDtypeStruct((DEVICES, DEVICES), BF16),
        ],
        in_specs=[pl.BlockSpec(memory_space=pltpu.SMEM), vm, vm, vm],
        out_specs=[vm, vm],
        name="tables",
    )(first, owner, policy, following)


def paths_kernel(core_ref, mine_ref, other_ref, out_ref, wide_ref):
    core = core_ref[0]
    for h, ref in enumerate((mine_ref, other_ref)):
        wide_ref[h] = ref[...].astype(F32)

    def field(h, row):
        return wide_ref[h, pl.ds(row, CHIPS, stride=TROWS), :]

    def full(base):
        return jnp.concatenate([field(h, base + r) for r in range(CAP) for h in range(2)], axis=0)

    n = 2 * CAP * CHIPS

    def places(shape, dim):
        i = iota(shape, dim)
        g, h, r = i & 63, lax.shift_right_logical(i, 6) & 1, lax.shift_right_logical(i, 7)
        return g, h, r, 2 * g + (h ^ core)

    def flag(x):
        return jnp.where(x, 1.0, 0.0).astype(BF16)

    half = SLOTS // 2
    g, h, r, s_row = places((n, DEVICES), 0)
    location = (h * CHIPS + g).astype(F32)
    s_f = s_row.astype(F32)
    s_loc_lane = 2 * (iota((n, DEVICES), 1) & 63) + (lax.shift_right_logical(iota((n, DEVICES), 1), 6) ^ core)
    lane = iota((n, DEVICES), 1)
    _, _, ra, sa = places((n, n), 0)
    _, _, rb, sb = places((n, n), 1)
    before = flag(sb * CAP + rb <= sa * CAP + ra)
    loc0 = iota((DEVICES, DEVICES), 0)
    s0 = 2 * (loc0 & 63) + (lax.shift_right_logical(loc0, 6) ^ core)
    d1 = iota((DEVICES, DEVICES), 1)
    turn = flag(s0 == d1)
    d_lane = iota((1, DEVICES), 1)
    d_f = d_lane.astype(F32)
    d_location = ((d_lane & 1) ^ core) * CHIPS + lax.shift_right_logical(d_lane, 1)

    spec = jnp.concatenate(
        [jnp.where(core == 0, field(k, COMMON), field(k, COMMON + 1)) for k in range(2)], axis=0
    )
    own = mm(spec, turn, TN)

    def mine(base):
        return own[base : base + CAP]

    totals = jnp.concatenate([field(0, 36), field(1, 36)], axis=0)
    offset = mm(flag(s_loc_lane < s_row), totals, NN) + half * s_f
    total = mm(flag(s_loc_lane == s_row), totals, NN) + half
    slot = full(0) + half
    kept = (slot < total) & (offset + slot < KEPT)
    count2 = jnp.where(kept, full(4), 0.0)
    cum2 = mm(before, count2, NN)
    ex2 = cum2 - count2
    total2 = jnp.minimum(jnp.sum(count2, axis=0, keepdims=True), float(SLOTS))
    total1_d = mm(totals, turn, TN)[0:1] + half
    offset1_d = mm(totals, flag(s0 < d1), TN)[0:1] + half * d_f
    j1 = mine(0) + half
    ok1 = (j1 < total1_d) & (offset1_d + j1 < KEPT)
    floc1 = d_location.astype(F32) * FRONT + mine(16)
    q1 = mine(8) * 16 + mine(12)
    wide2 = jnp.broadcast_to(total2 - half, (DEVICES, DEVICES))
    below = flag(loc0 < d1)
    less = flag(lane < s_row)
    same = flag(lane == s_row)
    offset = mm(less, wide2, NT) + half * s_f
    total = mm(same, wide2, NT) + half
    slot2 = full(20) + half
    kept = (slot2 < total) & (offset + slot2 < KEPT)
    count3 = jnp.where(kept, full(24), 0.0)
    cum3 = mm(before, count3, NN)
    ex3 = cum3 - count3
    total3 = jnp.minimum(jnp.sum(count3, axis=0, keepdims=True), float(SLOTS))
    j2 = mine(20) + half
    offset2_d = mm(wide2, below, NN)[0:1] + half * d_f
    ok2 = (j2 < total2) & (offset2_d + j2 < KEPT)
    parent1 = full(16)
    high1, low1 = full(8), full(12)
    path1 = (location * FRONT + parent1) * POLICY + high1 * 16 + low1
    path2 = []
    for r in range(CAP):
        j = j2[r : r + 1]
        path2.append(jnp.sum(jnp.where((ex2 <= j) & (j < cum2), path1, 0.0), axis=0, keepdims=True))
    path2 = jnp.concatenate(path2, axis=0).astype(I32)
    wide3 = jnp.broadcast_to(total3 - half, (DEVICES, DEVICES))
    offset3_d = mm(wide3, below, NN)[0:1] + half * d_f
    j3 = mine(36) + half
    ok3 = (j3 < total3) & (offset3_d + j3 < KEPT)
    policy2 = full(28) * 16 + full(32)
    via = s_f * 1024 + slot2
    stack = jnp.concatenate(
        [
            (jnp.minimum(cum2, float(SLOTS)) - half).astype(BF16),
            (jnp.minimum(ex2, float(SLOTS)) - half).astype(BF16),
            parent1.astype(BF16),
            high1.astype(BF16),
            low1.astype(BF16),
        ],
        axis=0,
    )
    path3, policy3 = [], []
    for r in range(CAP):
        j = j3[r : r + 1]
        hit = (ex3 <= j) & (j < cum3)
        policy3.append(jnp.sum(jnp.where(hit, policy2, 0.0), axis=0, keepdims=True))
        through = jnp.sum(jnp.where(hit, via, 0.0), axis=0, keepdims=True).astype(I32)
        device = lax.shift_right_logical(through, 10)
        jj = (through & 1023).astype(F32) - half
        got = mm(stack, flag(loc0 == device), NN)
        hit = (got[n : 2 * n] <= jj) & (jj < got[:n])
        path = (location * FRONT + got[2 * n : 3 * n]) * POLICY + got[3 * n : 4 * n] * 16 + got[4 * n :]
        path3.append(jnp.sum(jnp.where(hit, path, 0.0), axis=0, keepdims=True))
    path3 = jnp.concatenate(path3, axis=0).astype(I32)
    policy3 = jnp.concatenate(policy3, axis=0).astype(I32)

    def last(ok, base):
        return jnp.where(ok, (mine(base) * 16 + mine(base + 4)).astype(I32), POLICY)

    out_ref[0:4] = floc1.astype(I32)
    out_ref[4:8] = jnp.where(ok1, q1.astype(I32), POLICY)
    out_ref[8:12] = lax.shift_right_logical(path2, 11)
    out_ref[12:16] = path2 & (POLICY - 1)
    out_ref[16:20] = last(ok2, 28)
    out_ref[20:24] = lax.shift_right_logical(path3, 11)
    out_ref[24:28] = path3 & (POLICY - 1)
    out_ref[28:32] = policy3
    out_ref[32:36] = last(ok3, 40)
    out_ref[36:40] = jnp.zeros((4, DEVICES), I32)


def paths(core, mine, other):
    vm = pl.BlockSpec(memory_space=pltpu.VMEM)
    return pl.pallas_call(
        paths_kernel,
        out_shape=jax.ShapeDtypeStruct((40, DEVICES), I32),
        in_specs=[pl.BlockSpec(memory_space=pltpu.SMEM), vm, vm],
        out_specs=vm,
        scratch_shapes=[pltpu.VMEM((2, CHIPS * TROWS, 128), F32)],
        name="paths",
    )(core, mine, other)


FIELDS = ((0, (4,)), (8, (12, 16)), (20, (24, 28, 32)))


def values_kernel(
    paths_ref, mine_ref, other_ref, policy_ref, in_ref, out_w_ref, out_ref, front_ref, a_ref, b_ref, c_ref, x_ref, h_ref
):
    for half, ref in enumerate((mine_ref, other_ref)):

        @pl.loop(0, CHIPS)
        def _(i, half=half, ref=ref):
            at = pl.multiple_of((half * CHIPS + i) * FROWS, FROWS)
            front_ref[pl.ds(at, FROWS), :] = ref[i, :FROWS, :].astype(F32)

    def rows_of(table, index):
        at = index * CHUNKS
        return table[pl.ds(at, 8), :], table[pl.ds(at + 8, 8), :]

    def chunk(ref, start, k):
        return ref[pl.ds(start * STRIDE + k, 8, stride=STRIDE), :]

    for level in range(3):
        place, policies = FIELDS[level]
        hold = (a_ref, b_ref, c_ref)[: level + 1]
        for block in range(SLOTS // BLOCK):

            @pl.loop(0, BLOCK // 8)
            def _(i, block=block, place=place, policies=policies, hold=hold):
                for e in range(8):
                    s = block * (BLOCK // CAP) + i * 2 + e // CAP
                    r = e % CAP
                    at = pl.multiple_of((i * 8 + e) * STRIDE, STRIDE)
                    for k, (base, ref) in enumerate(zip(policies, hold)):
                        lo, hi = rows_of(policy_ref, paths_ref[base + r, s])
                        if k == 0:
                            flo, fhi = rows_of(front_ref, paths_ref[place + r, s])
                            lo, hi = lo * flo, hi * fhi
                        ref[pl.ds(at, 8), :] = lo
                        ref[pl.ds(pl.multiple_of(at + 8, 8), 8), :] = hi

            @pl.loop(0, BLOCK // 16)
            def _(i, block=block, hold=hold):
                child = [[None] * CHUNKS, [None] * CHUNKS]
                for u in range(2):
                    start = i * 16 + u * 8
                    for step, ref in enumerate(hold):
                        terms = [chunk(ref, start, k) for k in range(CHUNKS)]
                        if step:
                            terms = [t * c for t, c in zip(terms, child[u])]
                        mass = terms[0]
                        for t in terms[1:]:
                            mass = mass + t
                        mass = jnp.sum(mass, axis=1, keepdims=True)
                        scale = jnp.where(mass > 0, HANDS / mass, 0.0)
                        child[u] = [(t * scale).astype(BF16).astype(F32) for t in terms]
                at = pl.multiple_of(block * BLOCK + i * 16, 16)
                for k in range(CHUNKS):
                    both = jnp.concatenate([child[0][k], child[1][k]], axis=0).astype(BF16)
                    x_ref[pl.ds(at, 16), k * 128 : (k + 1) * 128] = both

        for block in range(2):
            rows = slice(block * 256, block * 256 + 256)
            for cut in range(0, HIDDEN, 512):
                hidden = jnp.dot(x_ref[rows, :], in_ref[:, cut : cut + 512], preferred_element_type=F32)
                h_ref[rows, cut : cut + 512] = jnp.maximum(hidden, 0.0).astype(BF16)
        for cut in range(0, HANDS, 256):
            end = min(cut + 256, HANDS)
            value = lax.dot_general(out_w_ref[cut:end, :], h_ref[...], (NT, ((), ())), preferred_element_type=F32)
            out_ref[level, cut:end, :] = value.astype(BF16)


def values(paths, mine, other, policy, value_in, value_out):
    vm = pl.BlockSpec(memory_space=pltpu.VMEM)
    hold = pltpu.VMEM((BLOCK * STRIDE, 128), F32)
    return pl.pallas_call(
        values_kernel,
        out_shape=jax.ShapeDtypeStruct((3, HANDS, SLOTS), BF16),
        in_specs=[pl.BlockSpec(memory_space=pltpu.SMEM), vm, vm, vm, vm, vm],
        out_specs=vm,
        scratch_shapes=[
            pltpu.VMEM((DEVICES * FROWS + 8, 128), F32),
            hold,
            hold,
            hold,
            pltpu.VMEM((SLOTS, WIDTH), BF16),
            pltpu.VMEM((SLOTS, HIDDEN), BF16),
        ],
        compiler_params=pltpu.CompilerParams(vmem_limit_bytes=62 * 1024 * 1024),
        name="values",
    )(paths, mine, other, policy, value_in, value_out)


def on_device(frontier, policy_table, first, policy_index, owner_index, following, value_in, value_out):
    core = lax.axis_index("owner_3").astype(I32)[None]
    common, spec = tables(first, owner_index, policy_index, following)
    ranges = jnp.pad(frontier, ((0, 0), (0, WIDTH - HANDS))).reshape(FROWS, 128)
    shared = jnp.concatenate([ranges, common[:COMMON]], axis=0)
    block = jnp.concatenate(
        [jnp.broadcast_to(shared[None], (CHIPS,) + shared.shape), spec.reshape(CHIPS, 2, 128)], axis=1
    )
    mine = lax.all_to_all(block, OWNER[:3], split_axis=0, concat_axis=0, tiled=True)
    other = lax.ppermute(mine, OWNER[3], [(0, 1), (1, 0)])
    policy = jnp.pad(policy_table, ((0, 1), (0, WIDTH - HANDS))).astype(F32).reshape((POLICY + 1) * CHUNKS, 128)
    policy = jnp.pad(policy, ((0, 13), (0, 0)))
    weights_in = jnp.pad(value_in, ((0, WIDTH - HANDS), (0, 0)))

    def part(x):
        return x[:, FROWS:, :].reshape(CHIPS * TROWS, 128)

    found = paths(core, part(mine), part(other))
    out = values(found, mine, other, policy, weights_in, jnp.transpose(value_out))
    return jnp.transpose(out, (0, 2, 1))


def solution(mesh):
    torus = Mesh(mesh.devices.reshape(4, 4, 4, 2), OWNER)
    placed = (P(OWNER, None), P(), P(OWNER), P(None, OWNER), P(None, OWNER), P(None, OWNER), P(), P())
    return jax.shard_map(on_device, mesh=torus, in_specs=placed, out_specs=P(None, OWNER, None), check_vma=False)
```

profile of v0, /device:TPU:1, one launch (start us, length us, event | category | flops | bytes accessed | tf_op | source)
XLA Modules:
  0.0 161.8 jit_solution(6262076183506545137)
XLA Ops:
  0.0 0.8 pad.18
  0.8 0.1 reshape.17
  0.9 2.8 %tables.1 = (bf16[40,128]{1,0:T(8,128)(2,1)}, bf16[128,128]{1,0:T(8,128)(2,1)}) custom-call(s32[16]{0:T(128)} %first_ref.1, s32[3,512]{1,0:T(4,128)} %owner_ref.1, s32[3,512]{1,0:T(4,128)} %policy_ref.1, s32[2,512]{1,0:T(2,128)} %next_ref.1), custom_call_target="tpu_custom_call" | custom-call | tf_op jit(solution)/shard_map/tables/pallas_call | solution.py:90
  3.7 0.7 pad_maximum_fusion.1
  4.4 0.5 broadcast_in_dim.10
  4.9 1.0 pad_maximum_fusion
  5.9 56.0 %all_to_all.5.mine_ref = bf16[64,216,128]{2,1,0:T(8,128)(2,1)S(1)} all-to-all(bf16[64,216,128]{2,1,0:T(8,128)(2,1)S(1)} %pad_maximum_fusion), channel_id=1, replica_groups=mesh['owner_0'=4,'owner_1'=4,'owner_2'=4,'owner_3'=2] {'owner_0','owner_..., dimensions={0} | all-to-all | bytes 7077888 | tf_op jit(solution)/shard_map/all_to_all | solution.py:343
  61.9 0.0 copy-start.1
  61.9 2.2 %collective-permute-start = (bf16[64,216,128]{2,1,0:T(8,128)(2,1)S(1)}, bf16[64,216,128]{2,1,0:T(8,128)(2,1)}, u32[]{:S(2)}, u32[]{:S(2)}) collective-permute-start(bf16[64,216,128]{2,1,0:T(8,128)(2,1)S(1)} %all_to_all.5.mine_ref), channel_id=1, source_target_pairs={{0,1},{1,0},{2,3},{3,2},{4,5},{5,4},{6,7},{7,6},{8,9},{9,8},{10,11... | collective-permute-start | bytes 10616840 | tf_op jit(solution)/shard_map/ppermute | solution.py:344
  64.1 8.2 %copy.10 = bf16[2048,1326]{1,0:T(8,128)(2,1)} copy(bf16[2048,1326]{0,1:T(8,128)(2,1)} %param.9) | data formatting | bytes 10862592
  72.4 5.6 %pad.19.clone = bf16[2049,1408]{1,0:T(8,128)(2,1)} pad(bf16[2048,1326]{1,0:T(8,128)(2,1)} %copy.10, bf16[]{:T(256)} %constant.8.clone.1), padding=0_1x0_82 | pad | bytes 11201282 | tf_op jit(solution)/shard_map/jit(_pad)/pad | solution.py:345
  77.9 11.8 %reshape.21 = bf16[22539,128]{1,0:T(8,128)(2,1)} reshape(bf16[2049,1408]{1,0:T(8,128)(2,1)} %pad.19.clone) | data formatting | bytes 11539968 | tf_op jit(solution)/shard_map/reshape | solution.py:345
  89.7 0.0 copy-start
  89.7 4.7 %pad.22.in_ref = bf16[1408,1536]{1,0:T(8,128)(2,1)} pad(bf16[1326,1536]{1,0:T(8,128)(2,1)} %param.14, bf16[]{:T(256)} %constant.8.clone.1), padding=0_82x0_0 | pad | bytes 8398850 | tf_op jit(solution)/shard_map/jit(_pad)/pad | solution.py:347
  94.4 0.0 copy-done
  94.4 5.1 %pad_convert_fusion.policy_ref = f32[22552,128]{1,0:T(8,128)} fusion(bf16[22539,128]{1,0:T(8,128)(2,1)S(1)} %copy-done), kind=kLoop, calls=%fused_computation | loop fusion | flops 2886656 | bytes 17316608 | tf_op jit(solution)/shard_map/jit(_pad)/pad | solution.py:346
  99.5 0.0 copy-done.1
  99.5 0.9 slice.12
  100.4 0.0 collective-permute-done.other_ref
  100.4 2.0 %slice.13 = bf16[64,40,128]{2,1,0:T(8,128)(2,1)} slice(bf16[64,216,128]{2,1,0:T(8,128)(2,1)} %collective-permute-done.other_ref), slice={[0:64], [176:216], [0:128]} | slice | bytes 1310720 | tf_op jit(solution)/shard_map/slice | solution.py:350
  102.4 4.4 %paths.1.paths_ref = s32[40,128]{1,0:T(8,128)} custom-call(s32[1]{0:T(128)} %bitcast.core_ref, bf16[2560,128]{1,0:T(8,128)(2,1)} %bitcast.8, bf16[2560,128]{1,0:T(8,128)(2,1)} %bitcast.9), custom_call_target="tpu_custom_call" | custom-call | tf_op jit(solution)/shard_map/paths/pallas_call | solution.py:234
  106.8 55.0 %values.1 = bf16[3,1326,512]{2,1,0:T(8,128)(2,1)} custom-call(s32[40,128]{1,0:T(8,128)} %paths.1.paths_ref, bf16[64,216,128]{2,1,0:T(8,128)(2,1)} %copy-done.1, bf16[64,216,128]{2,1,0:T(8,128)(2,1)} %collective-permute-done.other_ref, f32[22552,128]{1,0:T(8,128)} %pad_convert_fusion.policy_ref, bf16[1408,1536]{1,0:T(8,128)(2,1)} %pad.22.in_ref, ...), custom_call_target="tpu_custom_call" | custom-call | tf_op jit(solution)/shard_map/values/pallas_call | solution.py:317
Async XLA Ops:
  61.9 37.6 %copy-start.1 = (bf16[64,216,128]{2,1,0:T(8,128)(2,1)}, bf16[64,216,128]{2,1,0:T(8,128)(2,1)S(1)}, u32[]{:S(2)}) copy-start(bf16[64,216,128]{2,1,0:T(8,128)(2,1)S(1)} %all_to_all.5.mine_ref) | copy-start | bytes 10616836
  61.9 38.5 %collective-permute-start = (bf16[64,216,128]{2,1,0:T(8,128)(2,1)S(1)}, bf16[64,216,128]{2,1,0:T(8,128)(2,1)}, u32[]{:S(2)}, u32[]{:S(2)}) collective-permute-start(bf16[64,216,128]{2,1,0:T(8,128)(2,1)S(1)} %all_to_all.5.mine_ref), channel_id=1, source_target_pairs={{0,1},{1,0},{2,3},{3,2},{4,5},{5,4},{6,7},{7,6},{8,9},{9,8},{10,11... | collective-permute-start | bytes 10616840 | tf_op jit(solution)/shard_map/ppermute | solution.py:344
  89.7 4.7 %copy-start = (bf16[22539,128]{1,0:T(8,128)(2,1)S(1)}, bf16[22539,128]{1,0:T(8,128)(2,1)}, u32[]{:S(2)}) copy-start(bf16[22539,128]{1,0:T(8,128)(2,1)} %reshape.21) | copy-start | bytes 17309956
where the time goes:
time: 163 us; the launch traced here: 162 us
  Pallas kernels  62.2 us (38%)
  blocking collectives  56 us (34%)
  local copies, waits for them, and re-layouts  34.5 us (21%)
  other arithmetic  6.83 us (4%)
  starting transfers between devices  2.21 us (1%)
    all_to_all x1, blocking collectives, on_device(): lax.all_to_all(block, OWNER[:3], split_axis=0, concat_axis=0, tiled=True)  56 us
    pallas_call x1, Pallas kernels, values(): pl.pallas_call(values_kernel, out_shape=jax.ShapeDtypeStruct((3, HANDS, S...  55 us
    reshape x1, local copies, waits for them, and re-layouts, on_device(): jnp.pad(policy_table, ((0, 1), (0, WIDTH - HANDS))).astype(F32)  11.8 us
    unnamed x5, local copies, waits for them, and re-layouts  8.23 us
    pad x1, local copies, waits for them, and re-layouts, on_device(): jnp.pad(policy_table, ((0, 1), (0, WIDTH - HANDS))).astype(F32)  5.57 us
    pad x1, other arithmetic, on_device(): policy = jnp.pad(policy, ((0, 13), (0, 0)))  5.08 us
    pad x1, local copies, waits for them, and re-layouts, on_device(): weights_in = jnp.pad(value_in, ((0, WIDTH - HANDS), (0, 0)))  4.66 us
    pallas_call x1, Pallas kernels, paths(): pl.pallas_call(paths_kernel, out_shape=jax.ShapeDtypeStruct((40, DEVICES)...  4.38 us
  transfers between devices with their start and end apart: 1, of which 0 were waited for; matrix products, arithmetic and copies ran while one was open for 22% of the time, Pallas kernels for 0%

commit v1 on v0

--- a/solution.py
+++ b/solution.py
@@ -21,8 +21,9 @@
 COMMON = 38
 TROWS = COMMON + 2
 BROWS = FROWS + TROWS
-STRIDE = 16
+STRIDE = 17
 BLOCK = 256
+UNROLL = 64
 OWNER = ("owner_0", "owner_1", "owner_2", "owner_3")
 F32 = jnp.float32
 BF16 = jnp.bfloat16
@@ -245,7 +246,7 @@
 
 
 def values_kernel(
-    paths_ref, mine_ref, other_ref, policy_ref, in_ref, out_w_ref, out_ref, front_ref, a_ref, b_ref, c_ref, x_ref, h_ref
+    paths_ref, mine_ref, other_ref, policy_ref, in_ref, out_w_ref, out_ref, front_ref, a_ref, b_ref, c_ref, y_ref, x_ref, h_ref
 ):
     for half, ref in enumerate((mine_ref, other_ref)):
 
@@ -257,6 +258,9 @@
     def rows_of(table, index):
         at = index * CHUNKS
         return table[pl.ds(at, 8), :], table[pl.ds(at + 8, 8), :]
+
+    def rounded(t):
+        return t.astype(BF16).astype(F32)
 
     def chunk(ref, start, k):
         return ref[pl.ds(start * STRIDE + k, 8, stride=STRIDE), :]
@@ -271,34 +275,43 @@
                 for e in range(8):
                     s = block * (BLOCK // CAP) + i * 2 + e // CAP
                     r = e % CAP
-                    at = pl.multiple_of((i * 8 + e) * STRIDE, STRIDE)
+                    at = (i * 8 + e) * STRIDE
                     for k, (base, ref) in enumerate(zip(policies, hold)):
                         lo, hi = rows_of(policy_ref, paths_ref[base + r, s])
                         if k == 0:
                             flo, fhi = rows_of(front_ref, paths_ref[place + r, s])
                             lo, hi = lo * flo, hi * fhi
                         ref[pl.ds(at, 8), :] = lo
-                        ref[pl.ds(pl.multiple_of(at + 8, 8), 8), :] = hi
-
-            @pl.loop(0, BLOCK // 16)
+                        ref[pl.ds(at + 8, 8), :] = hi
+
+            @pl.loop(0, BLOCK // UNROLL)
             def _(i, block=block, hold=hold):
-                child = [[None] * CHUNKS, [None] * CHUNKS]
-                for u in range(2):
-                    start = i * 16 + u * 8
-                    for step, ref in enumerate(hold):
-                        terms = [chunk(ref, start, k) for k in range(CHUNKS)]
-                        if step:
-                            terms = [t * c for t, c in zip(terms, child[u])]
-                        mass = terms[0]
-                        for t in terms[1:]:
-                            mass = mass + t
-                        mass = jnp.sum(mass, axis=1, keepdims=True)
-                        scale = jnp.where(mass > 0, HANDS / mass, 0.0)
-                        child[u] = [(t * scale).astype(BF16).astype(F32) for t in terms]
-                at = pl.multiple_of(block * BLOCK + i * 16, 16)
-                for k in range(CHUNKS):
-                    both = jnp.concatenate([child[0][k], child[1][k]], axis=0).astype(BF16)
-                    x_ref[pl.ds(at, 16), k * 128 : (k + 1) * 128] = both
+                scales = [None] * (UNROLL // 8)
+                for step, ref in enumerate(hold):
+                    masses = []
+                    for u in range(UNROLL // 8):
+                        start = i * UNROLL + u * 8
+                        at = pl.ds(pl.multiple_of(start, 8), 8)
+                        mass = None
+                        for k in range(CHUNKS):
+                            term = chunk(ref, start, k)
+                            cut = slice(k * 128, (k + 1) * 128)
+                            if step:
+                                term = term * rounded(y_ref[at, cut] * scales[u])
+                            y_ref[at, cut] = term
+                            mass = term if mass is None else mass + term
+                        masses.append(mass)
+                    masses = [jnp.sum(m, axis=1, keepdims=True) for m in masses]
+                    scales = [jnp.where(m > 0, HANDS / m, 0.0) for m in masses]
+                for u in range(UNROLL // 16):
+                    start = i * UNROLL + u * 16
+                    at = pl.multiple_of(block * BLOCK + start, 16)
+                    for k in range(CHUNKS):
+                        cut = slice(k * 128, (k + 1) * 128)
+                        pair = [
+                            y_ref[pl.ds(pl.multiple_of(start + v * 8, 8), 8), cut] * scales[2 * u + v] for v in range(2)
+                        ]
+                        x_ref[pl.ds(at, 16), cut] = jnp.concatenate(pair, axis=0).astype(BF16)
 
         for block in range(2):
             rows = slice(block * 256, block * 256 + 256)
@@ -313,7 +326,7 @@
 
 def values(paths, mine, other, policy, value_in, value_out):
     vm = pl.BlockSpec(memory_space=pltpu.VMEM)
-    hold = pltpu.VMEM((BLOCK * STRIDE, 128), F32)
+    hold = pltpu.VMEM((BLOCK * STRIDE + 16, 128), F32)
     return pl.pallas_call(
         values_kernel,
         out_shape=jax.ShapeDtypeStruct((3, HANDS, SLOTS), BF16),
@@ -324,6 +337,7 @@
             hold,
             hold,
             hold,
+            pltpu.VMEM((BLOCK, WIDTH), F32),
             pltpu.VMEM((SLOTS, WIDTH), BF16),
             pltpu.VMEM((SLOTS, HIDDEN), BF16),
         ],
@@ -341,10 +355,11 @@
         [jnp.broadcast_to(shared[None], (CHIPS,) + shared.shape), spec.reshape(CHIPS, 2, 128)], axis=1
     )
     mine = lax.all_to_all(block, OWNER[:3], split_axis=0, concat_axis=0, tiled=True)
-    other = lax.ppermute(mine, OWNER[3], [(0, 1), (1, 0)])
     policy = jnp.pad(policy_table, ((0, 1), (0, WIDTH - HANDS))).astype(F32).reshape((POLICY + 1) * CHUNKS, 128)
     policy = jnp.pad(policy, ((0, 13), (0, 0)))
     weights_in = jnp.pad(value_in, ((0, WIDTH - HANDS), (0, 0)))
+    mine, policy, weights_in = lax.optimization_barrier((mine, policy, weights_in))
+    other = lax.ppermute(mine, OWNER[3], [(0, 1), (1, 0)])
 
     def part(x):
         return x[:, FROWS:, :].reshape(CHIPS * TROWS, 128)

time: 163 us -> 121 us (0.74)
  blocking collectives: 56 us -> 0 us
  Pallas kernels: 62.2 us -> 48.3 us
  starting transfers between devices: 2.21 us -> 14.8 us
  waiting for transfers between devices: 0.01 us -> 11.4 us
  other arithmetic: 6.83 us -> 11.2 us
    all_to_all x1 -> x0, blocking collectives: 56 us -> none  [on_device(): lax.all_to_all(block, OWNER[:3], split_axis=0, concat_axis=0, tiled=True)]
    pallas_call x1, Pallas kernels: 55 us -> 41.1 us  [values(): pl.pallas_call(values_kernel, out_shape=jax.ShapeDtypeStruct((3, HANDS, S...]
    all_to_all x0 -> x1, starting transfers between devices: none -> 12 us  [on_device(): lax.all_to_all(block, OWNER[:3], split_axis=0, concat_axis=0, tiled=True)]
    all_to_all x0 -> x1, waiting for transfers between devices: none -> 6.31 us  [on_device(): lax.all_to_all(block, OWNER[:3], split_axis=0, concat_axis=0, tiled=True)]
    ppermute x1, waiting for transfers between devices: 0.01 us -> 5.08 us  [on_device(): other = lax.ppermute(mine, OWNER[3], [(0, 1), (1, 0)])]
    pad x1, other arithmetic: 5.08 us -> 7.62 us  [on_device(): policy = jnp.pad(policy, ((0, 13), (0, 0)))]
    concatenate x1, other arithmetic: 1.04 us -> 2.83 us  [on_device(): jnp.concatenate([jnp.broadcast_to(shared[None], (CHIPS,) + shared.shape),...]
    unnamed x5 -> x3, local copies, waits for them, and re-layouts: 8.23 us -> 8.21 us
  transfers between devices with their start and end apart: 1 -> 2, of which waited for: 0 -> 2; matrix products, arithmetic and copies ran while one was open for 22% -> 32% of each run, Pallas kernels for 0% -> 0%
where the time goes in v1:
time: 121 us; the launch traced here: 120 us
  Pallas kernels  48.3 us (40%)
  local copies, waits for them, and re-layouts  34.3 us (28%)
  starting transfers between devices  14.8 us (12%)
  waiting for transfers between devices  11.4 us (9%)
  other arithmetic  11.2 us (9%)
    pallas_call x1, Pallas kernels, values(): pl.pallas_call(values_kernel, out_shape=jax.ShapeDtypeStruct((3, HANDS, S...  41.1 us
    all_to_all x1, starting transfers between devices, on_device(): lax.all_to_all(block, OWNER[:3], split_axis=0, concat_axis=0, tiled=True)  12 us
    reshape x1, local copies, waits for them, and re-layouts, on_device(): jnp.pad(policy_table, ((0, 1), (0, WIDTH - HANDS))).astype(F32)  11.8 us
    unnamed x3, local copies, waits for them, and re-layouts  8.21 us
    pad x1, other arithmetic, on_device(): policy = jnp.pad(policy, ((0, 13), (0, 0)))  7.62 us
    all_to_all x1, waiting for transfers between devices, on_device(): lax.all_to_all(block, OWNER[:3], split_axis=0, concat_axis=0, tiled=True)  6.31 us
    pad x1, local copies, waits for them, and re-layouts, on_device(): jnp.pad(policy_table, ((0, 1), (0, WIDTH - HANDS))).astype(F32)  5.55 us
    ppermute x1, waiting for transfers between devices, on_device(): other = lax.ppermute(mine, OWNER[3], [(0, 1), (1, 0)])  5.08 us
  transfers between devices with their start and end apart: 2, of which 2 were waited for; matrix products, arithmetic and copies ran while one was open for 32% of the time, Pallas kernels for 0%

profile of v1, /device:TPU:1, one launch (start us, length us, event | category | flops | bytes accessed | tf_op | source)
XLA Modules:
  0.0 120.0 jit_solution(11277675087114380693)
XLA Ops:
  0.0 0.8 pad.19
  0.8 0.1 reshape.17
  0.9 2.8 %tables.1 = (bf16[40,128]{1,0:T(8,128)(2,1)}, bf16[128,128]{1,0:T(8,128)(2,1)}) custom-call(s32[16]{0:T(128)} %first_ref.1, s32[3,512]{1,0:T(4,128)} %owner_ref.1, s32[3,512]{1,0:T(4,128)} %policy_ref.1, s32[2,512]{1,0:T(2,128)} %next_ref.1), custom_call_target="tpu_custom_call" | custom-call | tf_op jit(solution)/shard_map/tables/pallas_call | solution.py:91
  3.7 0.7 pad_maximum_fusion.1
  4.4 0.5 broadcast_in_dim.10
  4.9 2.8 %pad_maximum_fusion = bf16[64,216,128]{2,1,0:T(8,128)(2,1)} fusion(bf16[64,2,128]{2,1,0:T(2,128)(2,1)} %bitcast.10, bf16[64,214,128]{2,1,0:T(8,128)(2,1)S(1)} %broadcast_in_dim.10), kind=kLoop, calls=%fused_computation.1 | loop fusion | flops 7077888 | bytes 7077888 | tf_op jit(solution)/shard_map/concatenate | solution.py:354
  7.7 12.0 %all-to-all-start = ((bf16[64,216,128]{2,1,0:T(8,128)(2,1)}), bf16[64,216,128]{2,1,0:T(8,128)(2,1)S(1)}, u32[]{:S(2)}, u32[]{:S(2)}) async-start(bf16[64,216,128]{2,1,0:T(8,128)(2,1)} %pad_maximum_fusion), calls=%async_computation | async-start | bytes 7077888 | tf_op jit(solution)/shard_map/all_to_all | solution.py:357
  19.7 4.4 %pad.23.in_ref = bf16[1408,1536]{1,0:T(8,128)(2,1)} pad(bf16[1326,1536]{1,0:T(8,128)(2,1)} %param.14, bf16[]{:T(256)} %constant.8.clone.1), padding=0_82x0_0 | pad | bytes 8398850 | tf_op jit(solution)/shard_map/jit(_pad)/pad | solution.py:360
  24.1 8.2 %copy.10 = bf16[2048,1326]{1,0:T(8,128)(2,1)} copy(bf16[2048,1326]{0,1:T(8,128)(2,1)} %param.9) | data formatting | bytes 10862592
  32.3 5.6 %pad.20.clone = bf16[2049,1408]{1,0:T(8,128)(2,1)} pad(bf16[2048,1326]{1,0:T(8,128)(2,1)} %copy.10, bf16[]{:T(256)} %constant.8.clone.1), padding=0_1x0_82 | pad | bytes 11201282 | tf_op jit(solution)/shard_map/jit(_pad)/pad | solution.py:358
  37.8 11.8 %reshape.19 = bf16[22539,128]{1,0:T(8,128)(2,1)} reshape(bf16[2049,1408]{1,0:T(8,128)(2,1)} %pad.20.clone) | data formatting | bytes 11539968 | tf_op jit(solution)/shard_map/reshape | solution.py:358
  49.7 7.6 %pad_convert_fusion.policy_ref = f32[22552,128]{1,0:T(8,128)} fusion(bf16[22539,128]{1,0:T(8,128)(2,1)} %reshape.19), kind=kLoop, calls=%fused_computation | loop fusion | flops 2886656 | bytes 17316608 | tf_op jit(solution)/shard_map/jit(_pad)/pad | solution.py:359
  57.3 6.3 %all-to-all-done.mine_ref = bf16[64,216,128]{2,1,0:T(8,128)(2,1)S(1)} async-done(((bf16[64,216,128]{2,1,0:T(8,128)(2,1)}), bf16[64,216,128]{2,1,0:T(8,128)(2,1)S(1)}, u32[]{:S(2)}, u32[]{:S(2)}) %all-to-all-start) | async-done | bytes 3538976 | tf_op jit(solution)/shard_map/all_to_all | solution.py:357
  63.6 0.0 copy-start
  63.6 2.9 %collective-permute-start = (bf16[64,216,128]{2,1,0:T(8,128)(2,1)S(1)}, bf16[64,216,128]{2,1,0:T(8,128)(2,1)}, u32[]{:S(2)}, u32[]{:S(2)}) collective-permute-start(bf16[64,216,128]{2,1,0:T(8,128)(2,1)S(1)} %all-to-all-done.mine_ref), channel_id=1, source_target_pairs={{0,1},{1,0},{2,3},{3,2},{4,5},{5,4},{6,7},{7,6},{8,9},{9,8},{10,11... | collective-permute-start | bytes 10616840 | tf_op jit(solution)/shard_map/ppermute | solution.py:362
  66.5 0.0 copy-done
  66.5 0.9 slice.10
  67.4 5.1 %collective-permute-done.other_ref = bf16[64,216,128]{2,1,0:T(8,128)(2,1)} collective-permute-done((bf16[64,216,128]{2,1,0:T(8,128)(2,1)S(1)}, bf16[64,216,128]{2,1,0:T(8,128)(2,1)}, u32[]{:S(2)}, u32[]{:S(2)}) %collective-permute-start) | collective-permute-done | bytes 3538976 | tf_op jit(solution)/shard_map/ppermute | solution.py:362
  72.5 2.0 %slice.12 = bf16[64,40,128]{2,1,0:T(8,128)(2,1)} slice(bf16[64,216,128]{2,1,0:T(8,128)(2,1)} %collective-permute-done.other_ref), slice={[0:64], [176:216], [0:128]} | slice | bytes 1310720 | tf_op jit(solution)/shard_map/slice | solution.py:365
  74.5 4.4 %paths.1.paths_ref = s32[40,128]{1,0:T(8,128)} custom-call(s32[1]{0:T(128)} %bitcast.core_ref, bf16[2560,128]{1,0:T(8,128)(2,1)} %bitcast.8, bf16[2560,128]{1,0:T(8,128)(2,1)} %bitcast.9), custom_call_target="tpu_custom_call" | custom-call | tf_op jit(solution)/shard_map/paths/pallas_call | solution.py:235
  78.9 41.1 %values.1 = bf16[3,1326,512]{2,1,0:T(8,128)(2,1)} custom-call(s32[40,128]{1,0:T(8,128)} %paths.1.paths_ref, bf16[64,216,128]{2,1,0:T(8,128)(2,1)} %copy-done, bf16[64,216,128]{2,1,0:T(8,128)(2,1)} %collective-permute-done.other_ref, f32[22552,128]{1,0:T(8,128)} %pad_convert_fusion.policy_ref, bf16[1408,1536]{1,0:T(8,128)(2,1)} %pad.23.in_ref, ...), custom_call_target="tpu_custom_call" | custom-call | tf_op jit(solution)/shard_map/values/pallas_call | solution.py:330
Async XLA Ops:
  7.7 55.9 %all-to-all-start = ((bf16[64,216,128]{2,1,0:T(8,128)(2,1)}), bf16[64,216,128]{2,1,0:T(8,128)(2,1)S(1)}, u32[]{:S(2)}, u32[]{:S(2)}) async-start(bf16[64,216,128]{2,1,0:T(8,128)(2,1)} %pad_maximum_fusion), calls=%async_computation | async-start | bytes 7077888 | tf_op jit(solution)/shard_map/all_to_all | solution.py:357
  63.6 2.9 %copy-start = (bf16[64,216,128]{2,1,0:T(8,128)(2,1)}, bf16[64,216,128]{2,1,0:T(8,128)(2,1)S(1)}, u32[]{:S(2)}) copy-start(bf16[64,216,128]{2,1,0:T(8,128)(2,1)S(1)} %all-to-all-done.mine_ref) | copy-start | bytes 10616836
  63.6 8.9 %collective-permute-start = (bf16[64,216,128]{2,1,0:T(8,128)(2,1)S(1)}, bf16[64,216,128]{2,1,0:T(8,128)(2,1)}, u32[]{:S(2)}, u32[]{:S(2)}) collective-permute-start(bf16[64,216,128]{2,1,0:T(8,128)(2,1)S(1)} %all-to-all-done.mine_ref), channel_id=1, source_target_pairs={{0,1},{1,0},{2,3},{3,2},{4,5},{5,4},{6,7},{7,6},{8,9},{9,8},{10,11... | collective-permute-start | bytes 10616840 | tf_op jit(solution)/shard_map/ppermute | solution.py:362

commit v2 on v0

--- a/solution.py
+++ b/solution.py
@@ -21,8 +21,8 @@
 COMMON = 38
 TROWS = COMMON + 2
 BROWS = FROWS + TROWS
-STRIDE = 16
-BLOCK = 256
+STRIDE = 17
+UNROLL = 64
 OWNER = ("owner_0", "owner_1", "owner_2", "owner_3")
 F32 = jnp.float32
 BF16 = jnp.bfloat16
@@ -99,10 +99,10 @@
     )(first, owner, policy, following)
 
 
-def paths_kernel(core_ref, mine_ref, other_ref, out_ref, wide_ref):
-    core = core_ref[0]
-    for h, ref in enumerate((mine_ref, other_ref)):
-        wide_ref[h] = ref[...].astype(F32)
+def follow(core, table_ref, out_ref, wide_ref):
+    for h in range(2):
+        for i in range(CHIPS):
+            wide_ref[h, pl.ds(i * TROWS, TROWS), :] = table_ref[h, i].astype(F32)
 
     def field(h, row):
         return wide_ref[h, pl.ds(row, CHIPS, stride=TROWS), :]
@@ -229,107 +229,175 @@
     out_ref[36:40] = jnp.zeros((4, DEVICES), I32)
 
 
-def paths(core, mine, other):
-    vm = pl.BlockSpec(memory_space=pltpu.VMEM)
-    return pl.pallas_call(
-        paths_kernel,
-        out_shape=jax.ShapeDtypeStruct((40, DEVICES), I32),
-        in_specs=[pl.BlockSpec(memory_space=pltpu.SMEM), vm, vm],
-        out_specs=vm,
-        scratch_shapes=[pltpu.VMEM((2, CHIPS * TROWS, 128), F32)],
-        name="paths",
-    )(core, mine, other)
-
-
 FIELDS = ((0, (4,)), (8, (12, 16)), (20, (24, 28, 32)))
 
 
 def values_kernel(
-    paths_ref, mine_ref, other_ref, policy_ref, in_ref, out_w_ref, out_ref, front_ref, a_ref, b_ref, c_ref, x_ref, h_ref
+    core_ref,
+    mine_ref,
+    other_ref,
+    policy_hbm,
+    in_hbm,
+    out_w_hbm,
+    out_hbm,
+    table_ref,
+    wide_ref,
+    found_ref,
+    paths_ref,
+    ranges_ref,
+    front_ref,
+    policy_ref,
+    in_ref,
+    out_w_ref,
+    a_ref,
+    b_ref,
+    c_ref,
+    y_ref,
+    x0_ref,
+    x1_ref,
+    h_ref,
+    v0_ref,
+    v1_ref,
+    sems,
 ):
-    for half, ref in enumerate((mine_ref, other_ref)):
+    def load(src, dst, k):
+        copy = pltpu.make_async_copy(src, dst, sems.at[k])
+        copy.start()
+        return copy
+
+    halves = (mine_ref, other_ref)
+    table_loads = [load(ref.at[:, pl.ds(FROWS, TROWS), :], table_ref.at[k], k) for k, ref in enumerate(halves)]
+    range_loads = [load(ref.at[:, pl.ds(0, FROWS), :], ranges_ref.at[k], 2 + k) for k, ref in enumerate(halves)]
+    policy_load = load(policy_hbm, policy_ref, 4)
+    in_load = load(in_hbm, in_ref, 5)
+    out_w_load = load(out_w_hbm, out_w_ref, 6)
+    for copy in table_loads:
+        copy.wait()
+    follow(core_ref[0], table_ref, found_ref, wide_ref)
+    found_copy = load(found_ref, paths_ref, 7)
+    for half in range(2):
+        range_loads[half].wait()
 
         @pl.loop(0, CHIPS)
-        def _(i, half=half, ref=ref):
+        def _(i, half=half):
             at = pl.multiple_of((half * CHIPS + i) * FROWS, FROWS)
-            front_ref[pl.ds(at, FROWS), :] = ref[i, :FROWS, :].astype(F32)
+            front_ref[pl.ds(at, FROWS), :] = ranges_ref[half, i].astype(F32)
+
+    found_copy.wait()
+    policy_load.wait()
 
     def rows_of(table, index):
         at = index * CHUNKS
         return table[pl.ds(at, 8), :], table[pl.ds(at + 8, 8), :]
 
+    def rounded(t):
+        return t.astype(BF16).astype(F32)
+
     def chunk(ref, start, k):
         return ref[pl.ds(start * STRIDE + k, 8, stride=STRIDE), :]
 
-    for level in range(3):
+    def form(level, first, x_ref):
         place, policies = FIELDS[level]
         hold = (a_ref, b_ref, c_ref)[: level + 1]
-        for block in range(SLOTS // BLOCK):
-
-            @pl.loop(0, BLOCK // 8)
-            def _(i, block=block, place=place, policies=policies, hold=hold):
-                for e in range(8):
-                    s = block * (BLOCK // CAP) + i * 2 + e // CAP
-                    r = e % CAP
-                    at = pl.multiple_of((i * 8 + e) * STRIDE, STRIDE)
-                    for k, (base, ref) in enumerate(zip(policies, hold)):
-                        lo, hi = rows_of(policy_ref, paths_ref[base + r, s])
-                        if k == 0:
-                            flo, fhi = rows_of(front_ref, paths_ref[place + r, s])
-                            lo, hi = lo * flo, hi * fhi
-                        ref[pl.ds(at, 8), :] = lo
-                        ref[pl.ds(pl.multiple_of(at + 8, 8), 8), :] = hi
-
-            @pl.loop(0, BLOCK // 16)
-            def _(i, block=block, hold=hold):
-                child = [[None] * CHUNKS, [None] * CHUNKS]
-                for u in range(2):
-                    start = i * 16 + u * 8
-                    for step, ref in enumerate(hold):
-                        terms = [chunk(ref, start, k) for k in range(CHUNKS)]
-                        if step:
-                            terms = [t * c for t, c in zip(terms, child[u])]
-                        mass = terms[0]
-                        for t in terms[1:]:
-                            mass = mass + t
-                        mass = jnp.sum(mass, axis=1, keepdims=True)
-                        scale = jnp.where(mass > 0, HANDS / mass, 0.0)
-                        child[u] = [(t * scale).astype(BF16).astype(F32) for t in terms]
-                at = pl.multiple_of(block * BLOCK + i * 16, 16)
+        s0 = first // CAP if isinstance(first, int) else lax.shift_right_logical(first, 2)
+        for e in range(UNROLL):
+            s, r = s0 + e // CAP, e % CAP
+            for k, (base, ref) in enumerate(zip(policies, hold)):
+                lo, hi = rows_of(policy_ref, paths_ref[base + r, s])
+                if k == 0:
+                    flo, fhi = rows_of(front_ref, paths_ref[place + r, s])
+                    lo, hi = lo * flo, hi * fhi
+                ref[e * STRIDE : e * STRIDE + 8, :] = lo
+                ref[e * STRIDE + 8 : e * STRIDE + 16, :] = hi
+        scales = [None] * (UNROLL // 8)
+        for step, ref in enumerate(hold):
+            masses = []
+            for u in range(UNROLL // 8):
+                at = slice(u * 8, u * 8 + 8)
+                mass = None
                 for k in range(CHUNKS):
-                    both = jnp.concatenate([child[0][k], child[1][k]], axis=0).astype(BF16)
-                    x_ref[pl.ds(at, 16), k * 128 : (k + 1) * 128] = both
-
-        for block in range(2):
-            rows = slice(block * 256, block * 256 + 256)
-            for cut in range(0, HIDDEN, 512):
-                hidden = jnp.dot(x_ref[rows, :], in_ref[:, cut : cut + 512], preferred_element_type=F32)
-                h_ref[rows, cut : cut + 512] = jnp.maximum(hidden, 0.0).astype(BF16)
-        for cut in range(0, HANDS, 256):
-            end = min(cut + 256, HANDS)
-            value = lax.dot_general(out_w_ref[cut:end, :], h_ref[...], (NT, ((), ())), preferred_element_type=F32)
-            out_ref[level, cut:end, :] = value.astype(BF16)
-
-
-def values(paths, mine, other, policy, value_in, value_out):
-    vm = pl.BlockSpec(memory_space=pltpu.VMEM)
-    hold = pltpu.VMEM((BLOCK * STRIDE, 128), F32)
+                    term = chunk(ref, u * 8, k)
+                    cut = slice(k * 128, (k + 1) * 128)
+                    if step:
+                        term = term * rounded(y_ref[at, cut] * scales[u])
+                    y_ref[at, cut] = term
+                    mass = term if mass is None else mass + term
+                masses.append(mass)
+            masses = [jnp.sum(m, axis=1, keepdims=True) for m in masses]
+            scales = [jnp.where(m > 0, HANDS / m, 0.0) for m in masses]
+        for u in range(UNROLL // 16):
+            at = pl.multiple_of(first + u * 16, 16)
+            for k in range(CHUNKS):
+                cut = slice(k * 128, (k + 1) * 128)
+                pair = [y_ref[u * 16 + v * 8 : u * 16 + v * 8 + 8, cut] * scales[2 * u + v] for v in range(2)]
+                x_ref[pl.ds(at, 16), cut] = jnp.concatenate(pair, axis=0).astype(BF16)
+
+    @pl.loop(0, SLOTS // UNROLL)
+    def _(i):
+        form(0, i * UNROLL, x0_ref)
+
+    xs, vs, stores = (x0_ref, x1_ref), (v0_ref, v1_ref), [None, None]
+    in_load.wait()
+    out_w_load.wait()
+    for level in range(3):
+        x_ref, v_ref, ahead = xs[level % 2], vs[level % 2], xs[(level + 1) % 2]
+        if stores[level % 2] is not None:
+            stores[level % 2].wait()
+
+        for i in range(3):
+            if level < 2:
+                form(level + 1, i * UNROLL, ahead)
+            cut = slice(i * 512, i * 512 + 512)
+            hidden = jnp.dot(x_ref[...], in_ref[:, cut], preferred_element_type=F32)
+            h_ref[:, cut] = jnp.maximum(hidden, 0.0).astype(BF16)
+
+        def second(cut, v_ref=v_ref):
+            value = lax.dot_general(out_w_ref[cut, :], h_ref[...], (NT, ((), ())), preferred_element_type=F32)
+            v_ref[cut, :] = value.astype(BF16)
+
+        for i in range(5):
+            if level < 2:
+                form(level + 1, (i + 3) * UNROLL, ahead)
+            second(slice(i * 256, i * 256 + 256))
+
+        second(slice(1280, HANDS))
+        stores[level % 2] = load(v_ref, out_hbm.at[level], 8 + level % 2)
+    for copy in stores:
+        copy.wait()
+
+
+def values(core, mine, other, policy, value_in, value_out):
+    hbm = pl.BlockSpec(memory_space=pl.ANY)
+    hold = pltpu.VMEM((UNROLL * STRIDE + 16, 128), F32)
     return pl.pallas_call(
         values_kernel,
         out_shape=jax.ShapeDtypeStruct((3, HANDS, SLOTS), BF16),
-        in_specs=[pl.BlockSpec(memory_space=pltpu.SMEM), vm, vm, vm, vm, vm],
-        out_specs=vm,
+        in_specs=[pl.BlockSpec(memory_space=pltpu.SMEM), hbm, hbm, hbm, hbm, hbm],
+        out_specs=hbm,
         scratch_shapes=[
+            pltpu.VMEM((2, CHIPS, TROWS, 128), BF16),
+            pltpu.VMEM((2, CHIPS * TROWS, 128), F32),
+            pltpu.VMEM((40, 128), I32),
+            pltpu.SMEM((40, 128), I32),
+            pltpu.VMEM((2, CHIPS, FROWS, 128), BF16),
             pltpu.VMEM((DEVICES * FROWS + 8, 128), F32),
+            pltpu.VMEM(policy.shape, F32),
+            pltpu.VMEM((WIDTH, HIDDEN), BF16),
+            pltpu.VMEM((HANDS, HIDDEN), BF16),
             hold,
             hold,
             hold,
+            pltpu.VMEM((UNROLL, WIDTH), F32),
+            pltpu.VMEM((SLOTS, WIDTH), BF16),
             pltpu.VMEM((SLOTS, WIDTH), BF16),
             pltpu.VMEM((SLOTS, HIDDEN), BF16),
+            pltpu.VMEM((HANDS, SLOTS), BF16),
+            pltpu.VMEM((HANDS, SLOTS), BF16),
+            pltpu.SemaphoreType.DMA((10,)),
         ],
         compiler_params=pltpu.CompilerParams(vmem_limit_bytes=62 * 1024 * 1024),
         name="values",
-    )(paths, mine, other, policy, value_in, value_out)
+    )(core, mine, other, policy, value_in, value_out)
 
 
 def on_device(frontier, policy_table, first, policy_index, owner_index, following, value_in, value_out):
@@ -341,16 +409,13 @@
         [jnp.broadcast_to(shared[None], (CHIPS,) + shared.shape), spec.reshape(CHIPS, 2, 128)], axis=1
     )
     mine = lax.all_to_all(block, OWNER[:3], split_axis=0, concat_axis=0, tiled=True)
-    other = lax.ppermute(mine, OWNER[3], [(0, 1), (1, 0)])
     policy = jnp.pad(policy_table, ((0, 1), (0, WIDTH - HANDS))).astype(F32).reshape((POLICY + 1) * CHUNKS, 128)
     policy = jnp.pad(policy, ((0, 13), (0, 0)))
     weights_in = jnp.pad(value_in, ((0, WIDTH - HANDS), (0, 0)))
-
-    def part(x):
-        return x[:, FROWS:, :].reshape(CHIPS * TROWS, 128)
-
-    found = paths(core, part(mine), part(other))
-    out = values(found, mine, other, policy, weights_in, jnp.transpose(value_out))
+    mine, policy, weights_in = lax.optimization_barrier((mine, policy, weights_in))
+    other = lax.ppermute(mine, OWNER[3], [(0, 1), (1, 0)])
+
+    out = values(core, mine, other, policy, weights_in, jnp.transpose(value_out))
     return jnp.transpose(out, (0, 2, 1))
 
 

time: 163 us -> 105 us (0.64)
  blocking collectives: 56 us -> 0 us
  Pallas kernels: 62.2 us -> 32.6 us
  starting transfers between devices: 2.21 us -> 14.8 us
  waiting for transfers between devices: 0.01 us -> 12.3 us
  other arithmetic: 6.83 us -> 11.2 us
    all_to_all x1 -> x0, blocking collectives: 56 us -> none  [on_device(): lax.all_to_all(block, OWNER[:3], split_axis=0, concat_axis=0, tiled=True)]
    pallas_call x1, Pallas kernels: 55 us -> 29.8 us  [values(): pl.pallas_call(values_kernel, out_shape=jax.ShapeDtypeStruct((3, HANDS, S...]
    all_to_all x0 -> x1, starting transfers between devices: none -> 12 us  [on_device(): lax.all_to_all(block, OWNER[:3], split_axis=0, concat_axis=0, tiled=True)]
    all_to_all x0 -> x1, waiting for transfers between devices: none -> 6.31 us  [on_device(): lax.all_to_all(block, OWNER[:3], split_axis=0, concat_axis=0, tiled=True)]
    ppermute x1, waiting for transfers between devices: 0.01 us -> 5.98 us  [on_device(): other = lax.ppermute(mine, OWNER[3], [(0, 1), (1, 0)])]
    pallas_call x1 -> x0, Pallas kernels: 4.38 us -> none  [paths(): pl.pallas_call(paths_kernel, out_shape=jax.ShapeDtypeStruct((40, DEVICES)...]
    slice x2 -> x0, local copies, waits for them, and re-layouts: 2.9 us -> none  [part(): return x[:, FROWS:, :].reshape(CHIPS * TROWS, 128)]
    pad x1, other arithmetic: 5.08 us -> 7.62 us  [on_device(): policy = jnp.pad(policy, ((0, 13), (0, 0)))]
  transfers between devices with their start and end apart: 1 -> 2, of which waited for: 0 -> 2; matrix products, arithmetic and copies ran while one was open for 22% -> 36% of each run, Pallas kernels for 0% -> 0%
where the time goes in v2:
time: 105 us; the launch traced here: 104 us
  local copies, waits for them, and re-layouts  33.1 us (32%)
  Pallas kernels  32.6 us (31%)
  starting transfers between devices  14.8 us (14%)
  waiting for transfers between devices  12.3 us (12%)
  other arithmetic  11.2 us (11%)
    pallas_call x1, Pallas kernels, values(): pl.pallas_call(values_kernel, out_shape=jax.ShapeDtypeStruct((3, HANDS, S...  29.8 us
    all_to_all x1, starting transfers between devices, on_device(): lax.all_to_all(block, OWNER[:3], split_axis=0, concat_axis=0, tiled=True)  12 us
    reshape x1, local copies, waits for them, and re-layouts, on_device(): jnp.pad(policy_table, ((0, 1), (0, WIDTH - HANDS))).astype(F32)  11.8 us
    unnamed x3, local copies, waits for them, and re-layouts  9.99 us
    pad x1, other arithmetic, on_device(): policy = jnp.pad(policy, ((0, 13), (0, 0)))  7.62 us
    all_to_all x1, waiting for transfers between devices, on_device(): lax.all_to_all(block, OWNER[:3], split_axis=0, concat_axis=0, tiled=True)  6.31 us
    ppermute x1, waiting for transfers between devices, on_device(): other = lax.ppermute(mine, OWNER[3], [(0, 1), (1, 0)])  5.98 us
    pad x1, local copies, waits for them, and re-layouts, on_device(): jnp.pad(policy_table, ((0, 1), (0, WIDTH - HANDS))).astype(F32)  5.55 us
  transfers between devices with their start and end apart: 2, of which 2 were waited for; matrix products, arithmetic and copies ran while one was open for 36% of the time, Pallas kernels for 0%

profile of v2, /device:TPU:1, one launch (start us, length us, event | category | flops | bytes accessed | tf_op | source)
XLA Modules:
  0.0 104.2 jit_solution(17251990426877550705)
XLA Ops:
  0.0 0.8 pad.19
  0.8 0.1 reshape.11
  0.9 2.8 %tables.1 = (bf16[40,128]{1,0:T(8,128)(2,1)}, bf16[128,128]{1,0:T(8,128)(2,1)}) custom-call(s32[16]{0:T(128)} %first_ref.1, s32[3,512]{1,0:T(4,128)} %owner_ref.1, s32[3,512]{1,0:T(4,128)} %policy_ref.1, s32[2,512]{1,0:T(2,128)} %next_ref.1), custom_call_target="tpu_custom_call" | custom-call | tf_op jit(solution)/shard_map/tables/pallas_call | solution.py:90
  3.7 0.7 pad_maximum_fusion.1
  4.4 0.5 broadcast_in_dim.10
  4.9 2.8 %pad_maximum_fusion = bf16[64,216,128]{2,1,0:T(8,128)(2,1)} fusion(bf16[64,2,128]{2,1,0:T(2,128)(2,1)} %bitcast.6, bf16[64,214,128]{2,1,0:T(8,128)(2,1)S(1)} %broadcast_in_dim.10), kind=kLoop, calls=%fused_computation.1 | loop fusion | flops 7077888 | bytes 7077888 | tf_op jit(solution)/shard_map/concatenate | solution.py:408
  7.7 12.0 %all-to-all-start = ((bf16[64,216,128]{2,1,0:T(8,128)(2,1)}), bf16[64,216,128]{2,1,0:T(8,128)(2,1)S(1)}, u32[]{:S(2)}, u32[]{:S(2)}) async-start(bf16[64,216,128]{2,1,0:T(8,128)(2,1)} %pad_maximum_fusion), calls=%async_computation | async-start | bytes 7077888 | tf_op jit(solution)/shard_map/all_to_all | solution.py:411
  19.7 4.4 %pad.23.in_hbm = bf16[1408,1536]{1,0:T(8,128)(2,1)} pad(bf16[1326,1536]{1,0:T(8,128)(2,1)} %param.14, bf16[]{:T(256)} %constant.8.clone.1), padding=0_82x0_0 | pad | bytes 8398850 | tf_op jit(solution)/shard_map/jit(_pad)/pad | solution.py:414
  24.1 8.2 %copy.10 = bf16[2048,1326]{1,0:T(8,128)(2,1)} copy(bf16[2048,1326]{0,1:T(8,128)(2,1)} %param.9) | data formatting | bytes 10862592
  32.3 5.6 %pad.20.clone = bf16[2049,1408]{1,0:T(8,128)(2,1)} pad(bf16[2048,1326]{1,0:T(8,128)(2,1)} %copy.10, bf16[]{:T(256)} %constant.8.clone.1), padding=0_1x0_82 | pad | bytes 11201282 | tf_op jit(solution)/shard_map/jit(_pad)/pad | solution.py:412
  37.8 11.8 %reshape.13 = bf16[22539,128]{1,0:T(8,128)(2,1)} reshape(bf16[2049,1408]{1,0:T(8,128)(2,1)} %pad.20.clone) | data formatting | bytes 11539968 | tf_op jit(solution)/shard_map/reshape | solution.py:412
  49.7 7.6 %pad_convert_fusion.policy_hbm = f32[22552,128]{1,0:T(8,128)} fusion(bf16[22539,128]{1,0:T(8,128)(2,1)} %reshape.13), kind=kLoop, calls=%fused_computation | loop fusion | flops 2886656 | bytes 17316608 | tf_op jit(solution)/shard_map/jit(_pad)/pad | solution.py:413
  57.3 6.3 %all-to-all-done.mine_ref = bf16[64,216,128]{2,1,0:T(8,128)(2,1)S(1)} async-done(((bf16[64,216,128]{2,1,0:T(8,128)(2,1)}), bf16[64,216,128]{2,1,0:T(8,128)(2,1)S(1)}, u32[]{:S(2)}, u32[]{:S(2)}) %all-to-all-start) | async-done | bytes 3538976 | tf_op jit(solution)/shard_map/all_to_all | solution.py:411
  63.6 0.0 copy-start
  63.6 1.8 %copy-done = bf16[64,216,128]{2,1,0:T(8,128)(2,1)} copy-done((bf16[64,216,128]{2,1,0:T(8,128)(2,1)}, bf16[64,216,128]{2,1,0:T(8,128)(2,1)S(1)}, u32[]{:S(2)}) %copy-start) | copy-done | bytes 3538968
  65.4 2.9 %collective-permute-start = (bf16[64,216,128]{2,1,0:T(8,128)(2,1)S(1)}, bf16[64,216,128]{2,1,0:T(8,128)(2,1)}, u32[]{:S(2)}, u32[]{:S(2)}) collective-permute-start(bf16[64,216,128]{2,1,0:T(8,128)(2,1)S(1)} %all-to-all-done.mine_ref), channel_id=1, source_target_pairs={{0,1},{1,0},{2,3},{3,2},{4,5},{5,4},{6,7},{7,6},{8,9},{9,8},{10,11... | collective-permute-start | bytes 10616840 | tf_op jit(solution)/shard_map/ppermute | solution.py:416
  68.3 6.0 %collective-permute-done.other_ref = bf16[64,216,128]{2,1,0:T(8,128)(2,1)} collective-permute-done((bf16[64,216,128]{2,1,0:T(8,128)(2,1)S(1)}, bf16[64,216,128]{2,1,0:T(8,128)(2,1)}, u32[]{:S(2)}, u32[]{:S(2)}) %collective-permute-start) | collective-permute-done | bytes 3538976 | tf_op jit(solution)/shard_map/ppermute | solution.py:416
  74.3 29.8 %values.1 = bf16[3,1326,512]{2,1,0:T(8,128)(2,1)} custom-call(s32[1]{0:T(128)} %bitcast.core_ref, bf16[64,216,128]{2,1,0:T(8,128)(2,1)} %copy-done, bf16[64,216,128]{2,1,0:T(8,128)(2,1)} %collective-permute-done.other_ref, f32[22552,128]{1,0:T(8,128)} %pad_convert_fusion.policy_hbm, bf16[1408,1536]{1,0:T(8,128)(2,1)} %pad.23.in_hbm, bf16[1326,1536]{1,0:T(8,128)(2,1)} %bitcast.5), custom_call_target="tpu_custom_call" | custom-call | tf_op jit(solution)/shard_map/values/pallas_call | solution.py:372
Async XLA Ops:
  7.7 55.9 %all-to-all-start = ((bf16[64,216,128]{2,1,0:T(8,128)(2,1)}), bf16[64,216,128]{2,1,0:T(8,128)(2,1)S(1)}, u32[]{:S(2)}, u32[]{:S(2)}) async-start(bf16[64,216,128]{2,1,0:T(8,128)(2,1)} %pad_maximum_fusion), calls=%async_computation | async-start | bytes 7077888 | tf_op jit(solution)/shard_map/all_to_all | solution.py:411
  63.6 1.8 %copy-start = (bf16[64,216,128]{2,1,0:T(8,128)(2,1)}, bf16[64,216,128]{2,1,0:T(8,128)(2,1)S(1)}, u32[]{:S(2)}) copy-start(bf16[64,216,128]{2,1,0:T(8,128)(2,1)S(1)} %all-to-all-done.mine_ref) | copy-start | bytes 10616836
  65.4 8.9 %collective-permute-start = (bf16[64,216,128]{2,1,0:T(8,128)(2,1)S(1)}, bf16[64,216,128]{2,1,0:T(8,128)(2,1)}, u32[]{:S(2)}, u32[]{:S(2)}) collective-permute-start(bf16[64,216,128]{2,1,0:T(8,128)(2,1)S(1)} %all-to-all-done.mine_ref), channel_id=1, source_target_pairs={{0,1},{1,0},{2,3},{3,2},{4,5},{5,4},{6,7},{7,6},{8,9},{9,8},{10,11... | collective-permute-start | bytes 10616840 | tf_op jit(solution)/shard_map/ppermute | solution.py:416

commit v3 on v2

--- a/solution.py
+++ b/solution.py
@@ -17,9 +17,9 @@
 KEPT = 384 * DEVICES
 CHUNKS = 11
 WIDTH = CHUNKS * 128
-FROWS = FRONT * CHUNKS
-COMMON = 38
-TROWS = COMMON + 2
+FROWS = FRONT * (CHUNKS - 1) + FRONT // 2
+COMMON = 32
+TROWS = COMMON + 8
 BROWS = FROWS + TROWS
 STRIDE = 17
 UNROLL = 64
@@ -42,17 +42,25 @@
 TN = ((0,), (0,))
 
 
-def tables_kernel(first_ref, owner_ref, policy_ref, next_ref, common_ref, spec_ref):
+def tables_kernel(first_ref, owner_ref, policy_ref, next_ref, frontier_ref, out_hbm, block_ref, turn_ref, spec_ref, send_ref, sems):
+    for k in range(CHUNKS - 1):
+        block_ref[k * FRONT : (k + 1) * FRONT, :] = frontier_ref[:, k * 128 : (k + 1) * 128]
+    tail = frontier_ref[:, (CHUNKS - 1) * 128 :].astype(F32)
+    tail = jnp.concatenate([tail, jnp.zeros((FRONT, WIDTH - HANDS - 64), F32)], axis=1)
+    tail = jnp.concatenate([tail[:8], tail[8:]], axis=1)
     lane = iota((1, SLOTS), 1)
+    wide = iota((1, 128), 1)
     segment = jnp.zeros((1, SLOTS), I32)
+    ends = jnp.zeros((1, 128), I32)
     running = jnp.int32(0)
     for k in range(FRONT):
         running = running + first_ref[k]
+        ends = jnp.where(wide == 64 + k, jnp.minimum(running, SLOTS) - SLOTS // 2, ends)
         if k < FRONT - 1:
             segment = segment + (running <= lane).astype(I32)
-    total = jnp.minimum(running, SLOTS)
+    ends = jnp.where(wide == 80, jnp.minimum(running, SLOTS) - SLOTS // 2, ends)
     upper = (iota((SLOTS, SLOTS), 0) <= iota((SLOTS, SLOTS), 1)).astype(F32).astype(BF16)
-    rows = []
+    rows, own = [], []
     for level in range(3):
         hit = iota((DEVICES, SLOTS), 0) == owner_ref[level : level + 1, :]
         rank = mm(hit.astype(F32), upper, NN)
@@ -70,33 +78,44 @@
         low = [f[3:4] for f in found]
         count = [f[4:5] for f in found]
         parent = [f[5:6] for f in found]
-        if level == 0:
-            rows += slot + count + high + low + parent
-        elif level == 1:
+        if level < 2:
             rows += slot + count + high + low
-        else:
-            last = slot + high + low
-    lanes = jnp.zeros((1, DEVICES), F32)
-    zero = [lanes]
-    common = rows + [lanes + (total - SLOTS // 2).astype(F32)] + zero
-    common = jnp.concatenate(common + zero * (40 - len(common)), axis=0)
-    common_ref[...] = common.astype(BF16)
-    spec = jnp.concatenate(rows + last + zero * (DEVICES - len(rows) - len(last)), axis=0)
-    spec_ref[...] = jnp.transpose(spec).astype(BF16)
-
-
-def tables(first, owner, policy, following):
+        own += slot + high + low + (parent if level == 0 else [])
+    block_ref[FROWS - 8 :, :] = jnp.concatenate([tail] + rows, axis=0).astype(BF16)
+    copies = [
+        pltpu.make_async_copy(block_ref, out_hbm.at[i, pl.ds(0, FROWS + COMMON), :], sems.at[0]) for i in range(CHIPS)
+    ]
+    for copy in copies:
+        copy.start()
+    zero = [jnp.zeros((1, DEVICES), F32)]
+    turn_ref[...] = jnp.transpose(jnp.concatenate(own + zero * (DEVICES - len(own)), axis=0)) + ends.astype(F32)
+    spec_ref[...] = jnp.zeros((CHIPS * 8, 128), F32)
+    for c in range(2):
+        spec_ref[pl.ds(c, CHIPS, stride=8), :] = turn_ref[pl.ds(c, CHIPS, stride=2), :]
+    send_ref[...] = spec_ref[...].astype(BF16).reshape(CHIPS, 8, 128)
+    last = pltpu.make_async_copy(send_ref, out_hbm.at[:, pl.ds(FROWS + COMMON, 8), :], sems.at[1])
+    last.start()
+    for copy in copies:
+        copy.wait()
+    last.wait()
+
+
+def tables(first, owner, policy, following, frontier):
     vm = pl.BlockSpec(memory_space=pltpu.VMEM)
     return pl.pallas_call(
         tables_kernel,
-        out_shape=[
-            jax.ShapeDtypeStruct((40, DEVICES), BF16),
-            jax.ShapeDtypeStruct((DEVICES, DEVICES), BF16),
+        out_shape=jax.ShapeDtypeStruct((CHIPS, BROWS, 128), BF16),
+        in_specs=[pl.BlockSpec(memory_space=pltpu.SMEM), vm, vm, vm, vm],
+        out_specs=pl.BlockSpec(memory_space=pl.ANY),
+        scratch_shapes=[
+            pltpu.VMEM((FROWS + COMMON, 128), BF16),
+            pltpu.VMEM((DEVICES, 128), F32),
+            pltpu.VMEM((CHIPS * 8, 128), F32),
+            pltpu.VMEM((CHIPS, 8, 128), BF16),
+            pltpu.SemaphoreType.DMA((2,)),
         ],
-        in_specs=[pl.BlockSpec(memory_space=pltpu.SMEM), vm, vm, vm],
-        out_specs=[vm, vm],
         name="tables",
-    )(first, owner, policy, following)
+    )(first, owner, policy, following, frontier)
 
 
 def follow(core, table_ref, out_ref, wide_ref):
@@ -145,10 +164,15 @@
     def mine(base):
         return own[base : base + CAP]
 
-    totals = jnp.concatenate([field(0, 36), field(1, 36)], axis=0)
+    totals = jnp.broadcast_to(spec[:, 80:81], (DEVICES, DEVICES))
     offset = mm(flag(s_loc_lane < s_row), totals, NN) + half * s_f
     total = mm(flag(s_loc_lane == s_row), totals, NN) + half
-    slot = full(0) + half
+    slot1 = full(0)
+    parent1 = jnp.zeros((n, DEVICES), F32)
+    for k in range(FRONT - 1):
+        ends = jnp.broadcast_to(spec[:, 64 + k : 65 + k], (DEVICES, DEVICES))
+        parent1 = parent1 + jnp.where(jnp.concatenate([ends] * CAP, axis=0) <= slot1, 1.0, 0.0)
+    slot = slot1 + half
     kept = (slot < total) & (offset + slot < KEPT)
     count2 = jnp.where(kept, full(4), 0.0)
     cum2 = mm(before, count2, NN)
@@ -158,24 +182,23 @@
     offset1_d = mm(totals, flag(s0 < d1), TN)[0:1] + half * d_f
     j1 = mine(0) + half
     ok1 = (j1 < total1_d) & (offset1_d + j1 < KEPT)
-    floc1 = d_location.astype(F32) * FRONT + mine(16)
-    q1 = mine(8) * 16 + mine(12)
+    floc1 = d_location.astype(F32) * FRONT + mine(12)
+    q1 = mine(4) * 16 + mine(8)
     wide2 = jnp.broadcast_to(total2 - half, (DEVICES, DEVICES))
     below = flag(loc0 < d1)
     less = flag(lane < s_row)
     same = flag(lane == s_row)
     offset = mm(less, wide2, NT) + half * s_f
     total = mm(same, wide2, NT) + half
-    slot2 = full(20) + half
+    slot2 = full(16) + half
     kept = (slot2 < total) & (offset + slot2 < KEPT)
-    count3 = jnp.where(kept, full(24), 0.0)
+    count3 = jnp.where(kept, full(20), 0.0)
     cum3 = mm(before, count3, NN)
     ex3 = cum3 - count3
     total3 = jnp.minimum(jnp.sum(count3, axis=0, keepdims=True), float(SLOTS))
-    j2 = mine(20) + half
+    j2 = mine(16) + half
     offset2_d = mm(wide2, below, NN)[0:1] + half * d_f
     ok2 = (j2 < total2) & (offset2_d + j2 < KEPT)
-    parent1 = full(16)
     high1, low1 = full(8), full(12)
     path1 = (location * FRONT + parent1) * POLICY + high1 * 16 + low1
     path2 = []
@@ -185,9 +208,9 @@
     path2 = jnp.concatenate(path2, axis=0).astype(I32)
     wide3 = jnp.broadcast_to(total3 - half, (DEVICES, DEVICES))
     offset3_d = mm(wide3, below, NN)[0:1] + half * d_f
-    j3 = mine(36) + half
+    j3 = mine(28) + half
     ok3 = (j3 < total3) & (offset3_d + j3 < KEPT)
-    policy2 = full(28) * 16 + full(32)
+    policy2 = full(24) * 16 + full(28)
     via = s_f * 1024 + slot2
     stack = jnp.concatenate(
         [
@@ -221,11 +244,11 @@
     out_ref[4:8] = jnp.where(ok1, q1.astype(I32), POLICY)
     out_ref[8:12] = lax.shift_right_logical(path2, 11)
     out_ref[12:16] = path2 & (POLICY - 1)
-    out_ref[16:20] = last(ok2, 28)
+    out_ref[16:20] = last(ok2, 20)
     out_ref[20:24] = lax.shift_right_logical(path3, 11)
     out_ref[24:28] = path3 & (POLICY - 1)
     out_ref[28:32] = policy3
-    out_ref[32:36] = last(ok3, 40)
+    out_ref[32:36] = last(ok3, 32)
     out_ref[36:40] = jnp.zeros((4, DEVICES), I32)
 
 
@@ -278,10 +301,17 @@
     for half in range(2):
         range_loads[half].wait()
 
-        @pl.loop(0, CHIPS)
-        def _(i, half=half):
-            at = pl.multiple_of((half * CHIPS + i) * FROWS, FROWS)
-            front_ref[pl.ds(at, FROWS), :] = ranges_ref[half, i].astype(F32)
+        @pl.loop(0, CHIPS // 16)
+        def _(j, half=half):
+            for e in range(16):
+                i = j * 16 + e
+                at = (half * CHIPS + i) * (FRONT * CHUNKS)
+                for k in range(CHUNKS - 1):
+                    wide = ranges_ref[half, i, k * FRONT : (k + 1) * FRONT].astype(F32)
+                    front_ref[pl.ds(at + k, FRONT, stride=CHUNKS), :] = wide
+                tail = ranges_ref[half, i, FROWS - 8 : FROWS].astype(F32)
+                front_ref[pl.ds(at + CHUNKS - 1, 8, stride=CHUNKS), :] = tail
+                front_ref[pl.ds(at + 9 * CHUNKS - 1, 8, stride=CHUNKS), :] = pltpu.roll(tail, 64, 1)
 
     found_copy.wait()
     policy_load.wait()
@@ -380,7 +410,7 @@
             pltpu.VMEM((40, 128), I32),
             pltpu.SMEM((40, 128), I32),
             pltpu.VMEM((2, CHIPS, FROWS, 128), BF16),
-            pltpu.VMEM((DEVICES * FROWS + 8, 128), F32),
+            pltpu.VMEM((DEVICES * FRONT * CHUNKS + 8, 128), F32),
             pltpu.VMEM(policy.shape, F32),
             pltpu.VMEM((WIDTH, HIDDEN), BF16),
             pltpu.VMEM((HANDS, HIDDEN), BF16),
@@ -402,12 +432,7 @@
 
 def on_device(frontier, policy_table, first, policy_index, owner_index, following, value_in, value_out):
     core = lax.axis_index("owner_3").astype(I32)[None]
-    common, spec = tables(first, owner_index, policy_index, following)
-    ranges = jnp.pad(frontier, ((0, 0), (0, WIDTH - HANDS))).reshape(FROWS, 128)
-    shared = jnp.concatenate([ranges, common[:COMMON]], axis=0)
-    block = jnp.concatenate(
-        [jnp.broadcast_to(shared[None], (CHIPS,) + shared.shape), spec.reshape(CHIPS, 2, 128)], axis=1
-    )
+    block = tables(first, owner_index, policy_index, following, frontier)
     mine = lax.all_to_all(block, OWNER[:3], split_axis=0, concat_axis=0, tiled=True)
     policy = jnp.pad(policy_table, ((0, 1), (0, WIDTH - HANDS))).astype(F32).reshape((POLICY + 1) * CHUNKS, 128)
     policy = jnp.pad(policy, ((0, 13), (0, 0)))

time: 105 us -> 99.4 us (0.947)
  local copies, waits for them, and re-layouts: 33.1 us -> 29.3 us
  other arithmetic: 11.2 us -> 7.62 us
    concatenate x2 -> x0, other arithmetic: 3.54 us -> none  [the longest x1 2.83 us: on_device(): jnp.concatenate([jnp.broadcast_to(shared[None], (CHIPS,) + shared.shape),...]
    pad x1, local copies, waits for them, and re-layouts: 5.55 us -> 2.92 us  [on_device(): jnp.pad(policy_table, ((0, 1), (0, WIDTH - HANDS))).astype(F32)]
    pallas_call x1, Pallas kernels: 2.81 us -> 3.88 us  [tables(): pl.pallas_call(tables_kernel, out_shape=jax.ShapeDtypeStruct((CHIPS, BROW...]
    unnamed x3 -> x5, local copies, waits for them, and re-layouts: 9.99 us -> 9.93 us
where the time goes in v3:
time: 99.4 us; the launch traced here: 98.6 us
  Pallas kernels  33.6 us (34%)
  local copies, waits for them, and re-layouts  29.3 us (29%)
  starting transfers between devices  14.9 us (15%)
  waiting for transfers between devices  13 us (13%)
  other arithmetic  7.62 us (8%)
    pallas_call x1, Pallas kernels, values(): pl.pallas_call(values_kernel, out_shape=jax.ShapeDtypeStruct((3, HANDS, S...  29.7 us
    all_to_all x1, starting transfers between devices, on_device(): lax.all_to_all(block, OWNER[:3], split_axis=0, concat_axis=0, tiled=True)  12 us
    reshape x1, local copies, waits for them, and re-layouts, on_device(): jnp.pad(policy_table, ((0, 1), (0, WIDTH - HANDS))).astype(F32)  11.8 us
    unnamed x5, local copies, waits for them, and re-layouts  9.93 us
    pad x1, other arithmetic, on_device(): policy = jnp.pad(policy, ((0, 13), (0, 0)))  7.62 us
    all_to_all x1, waiting for transfers between devices, on_device(): lax.all_to_all(block, OWNER[:3], split_axis=0, concat_axis=0, tiled=True)  7.25 us
    ppermute x1, waiting for transfers between devices, on_device(): other = lax.ppermute(mine, OWNER[3], [(0, 1), (1, 0)])  5.79 us
    pad x1, local copies, waits for them, and re-layouts, on_device(): weights_in = jnp.pad(value_in, ((0, WIDTH - HANDS), (0, 0)))  4.58 us
  transfers between devices with their start and end apart: 2, of which 2 were waited for; matrix products, arithmetic and copies ran while one was open for 36% of the time, Pallas kernels for 0%

profile of v3, /device:TPU:1, one launch (start us, length us, event | category | flops | bytes accessed | tf_op | source)
XLA Modules:
  0.0 98.6 jit_solution(5433679978912982960)
XLA Ops:
  0.0 3.9 %tables.1 = bf16[64,208,128]{2,1,0:T(8,128)(2,1)} custom-call(s32[16]{0:T(128)} %first_ref.1, s32[3,512]{1,0:T(4,128)} %owner_ref.1, s32[3,512]{1,0:T(4,128)} %policy_ref.1, s32[2,512]{1,0:T(2,128)} %next_ref.1, bf16[16,1326]{1,0:T(8,128)(2,1)} %frontier_ref.1), custom_call_target="tpu_custom_call" | custom-call | tf_op jit(solution)/shard_map/tables/pallas_call | solution.py:105
  3.9 12.0 %all-to-all-start = ((bf16[64,208,128]{2,1,0:T(8,128)(2,1)}), bf16[64,208,128]{2,1,0:T(8,128)(2,1)S(1)}, u32[]{:S(2)}, u32[]{:S(2)}) async-start(bf16[64,208,128]{2,1,0:T(8,128)(2,1)} %tables.1), calls=%async_computation | async-start | bytes 6815744 | tf_op jit(solution)/shard_map/all_to_all | solution.py:436
  15.9 8.2 %copy.10 = bf16[2048,1326]{1,0:T(8,128)(2,1)} copy(bf16[2048,1326]{0,1:T(8,128)(2,1)} %param.9) | data formatting | bytes 10862592
  24.0 0.0 copy-start
  24.0 4.6 %pad.18.in_hbm = bf16[1408,1536]{1,0:T(8,128)(2,1)} pad(bf16[1326,1536]{1,0:T(8,128)(2,1)} %param.14, bf16[]{:T(256)} %constant.8.clone.1), padding=0_82x0_0 | pad | bytes 8398850 | tf_op jit(solution)/shard_map/jit(_pad)/pad | solution.py:439
  28.6 0.0 copy-done
  28.6 2.9 %pad.15.clone = bf16[2049,1408]{1,0:T(8,128)(2,1)} pad(bf16[2048,1326]{1,0:T(8,128)(2,1)S(1)} %copy-done, bf16[]{:T(256)} %constant.8.clone.1), padding=0_1x0_82 | pad | bytes 11201282 | tf_op jit(solution)/shard_map/jit(_pad)/pad | solution.py:437
  31.6 11.8 %reshape.4 = bf16[22539,128]{1,0:T(8,128)(2,1)} reshape(bf16[2049,1408]{1,0:T(8,128)(2,1)} %pad.15.clone) | data formatting | bytes 11539968 | tf_op jit(solution)/shard_map/reshape | solution.py:437
  43.4 7.6 %pad_convert_fusion.policy_hbm = f32[22552,128]{1,0:T(8,128)} fusion(bf16[22539,128]{1,0:T(8,128)(2,1)} %reshape.4), kind=kLoop, calls=%fused_computation | loop fusion | flops 2886656 | bytes 17316608 | tf_op jit(solution)/shard_map/jit(_pad)/pad | solution.py:438
  51.0 7.3 %all-to-all-done.mine_ref = bf16[64,208,128]{2,1,0:T(8,128)(2,1)S(1)} async-done(((bf16[64,208,128]{2,1,0:T(8,128)(2,1)}), bf16[64,208,128]{2,1,0:T(8,128)(2,1)S(1)}, u32[]{:S(2)}, u32[]{:S(2)}) %all-to-all-start) | async-done | bytes 3407904 | tf_op jit(solution)/shard_map/all_to_all | solution.py:436
  58.3 0.0 copy-start.1
  58.3 1.7 %copy-done.1 = bf16[64,208,128]{2,1,0:T(8,128)(2,1)} copy-done((bf16[64,208,128]{2,1,0:T(8,128)(2,1)}, bf16[64,208,128]{2,1,0:T(8,128)(2,1)S(1)}, u32[]{:S(2)}) %copy-start.1) | copy-done | bytes 3407896
  60.0 3.0 %collective-permute-start = (bf16[64,208,128]{2,1,0:T(8,128)(2,1)S(1)}, bf16[64,208,128]{2,1,0:T(8,128)(2,1)}, u32[]{:S(2)}, u32[]{:S(2)}) collective-permute-start(bf16[64,208,128]{2,1,0:T(8,128)(2,1)S(1)} %all-to-all-done.mine_ref), channel_id=1, source_target_pairs={{0,1},{1,0},{2,3},{3,2},{4,5},{5,4},{6,7},{7,6},{8,9},{9,8},{10,11... | collective-permute-start | bytes 10223624 | tf_op jit(solution)/shard_map/ppermute | solution.py:441
  63.0 5.8 %collective-permute-done.other_ref = bf16[64,208,128]{2,1,0:T(8,128)(2,1)} collective-permute-done((bf16[64,208,128]{2,1,0:T(8,128)(2,1)S(1)}, bf16[64,208,128]{2,1,0:T(8,128)(2,1)}, u32[]{:S(2)}, u32[]{:S(2)}) %collective-permute-start) | collective-permute-done | bytes 3407904 | tf_op jit(solution)/shard_map/ppermute | solution.py:441
  68.8 29.7 %values.1 = bf16[3,1326,512]{2,1,0:T(8,128)(2,1)} custom-call(s32[1]{0:T(128)} %bitcast.core_ref, bf16[64,208,128]{2,1,0:T(8,128)(2,1)} %copy-done.1, bf16[64,208,128]{2,1,0:T(8,128)(2,1)} %collective-permute-done.other_ref, f32[22552,128]{1,0:T(8,128)} %pad_convert_fusion.policy_hbm, bf16[1408,1536]{1,0:T(8,128)(2,1)} %pad.18.in_hbm, bf16[1326,1536]{1,0:T(8,128)(2,1)} %bitcast.3), custom_call_target="tpu_custom_call" | custom-call | tf_op jit(solution)/shard_map/values/pallas_call | solution.py:402
Async XLA Ops:
  3.9 54.4 %all-to-all-start = ((bf16[64,208,128]{2,1,0:T(8,128)(2,1)}), bf16[64,208,128]{2,1,0:T(8,128)(2,1)S(1)}, u32[]{:S(2)}, u32[]{:S(2)}) async-start(bf16[64,208,128]{2,1,0:T(8,128)(2,1)} %tables.1), calls=%async_computation | async-start | bytes 6815744 | tf_op jit(solution)/shard_map/all_to_all | solution.py:436
  24.0 4.6 %copy-start = (bf16[2048,1326]{1,0:T(8,128)(2,1)S(1)}, bf16[2048,1326]{1,0:T(8,128)(2,1)}, u32[]{:S(2)}) copy-start(bf16[2048,1326]{1,0:T(8,128)(2,1)} %copy.10) | copy-start | bytes 16293892
  58.3 1.7 %copy-start.1 = (bf16[64,208,128]{2,1,0:T(8,128)(2,1)}, bf16[64,208,128]{2,1,0:T(8,128)(2,1)S(1)}, u32[]{:S(2)}) copy-start(bf16[64,208,128]{2,1,0:T(8,128)(2,1)S(1)} %all-to-all-done.mine_ref) | copy-start | bytes 10223620
  60.0 8.8 %collective-permute-start = (bf16[64,208,128]{2,1,0:T(8,128)(2,1)S(1)}, bf16[64,208,128]{2,1,0:T(8,128)(2,1)}, u32[]{:S(2)}, u32[]{:S(2)}) collective-permute-start(bf16[64,208,128]{2,1,0:T(8,128)(2,1)S(1)} %all-to-all-done.mine_ref), channel_id=1, source_target_pairs={{0,1},{1,0},{2,3},{3,2},{4,5},{5,4},{6,7},{7,6},{8,9},{9,8},{10,11... | collective-permute-start | bytes 10223624 | tf_op jit(solution)/shard_map/ppermute | solution.py:441

commit v4 on v3

--- a/solution.py
+++ b/solution.py
@@ -17,8 +17,11 @@
 KEPT = 384 * DEVICES
 CHUNKS = 11
 WIDTH = CHUNKS * 128
-FROWS = FRONT * (CHUNKS - 1) + FRONT // 2
+FROWS = FRONT * (CHUNKS - 1)
 COMMON = 32
+ENDS = 44
+PIECE = 18
+SPARE = (46, 110)
 TROWS = COMMON + 8
 BROWS = FROWS + TROWS
 STRIDE = 17
@@ -55,10 +58,10 @@
     running = jnp.int32(0)
     for k in range(FRONT):
         running = running + first_ref[k]
-        ends = jnp.where(wide == 64 + k, jnp.minimum(running, SLOTS) - SLOTS // 2, ends)
+        ends = jnp.where(wide == ENDS + k, jnp.minimum(running, SLOTS) - SLOTS // 2, ends)
         if k < FRONT - 1:
             segment = segment + (running <= lane).astype(I32)
-    ends = jnp.where(wide == 80, jnp.minimum(running, SLOTS) - SLOTS // 2, ends)
+    ends = jnp.where(wide == ENDS + FRONT, jnp.minimum(running, SLOTS) - SLOTS // 2, ends)
     upper = (iota((SLOTS, SLOTS), 0) <= iota((SLOTS, SLOTS), 1)).astype(F32).astype(BF16)
     rows, own = [], []
     for level in range(3):
@@ -81,7 +84,7 @@
         if level < 2:
             rows += slot + count + high + low
         own += slot + high + low + (parent if level == 0 else [])
-    block_ref[FROWS - 8 :, :] = jnp.concatenate([tail] + rows, axis=0).astype(BF16)
+    block_ref[FROWS:, :] = jnp.concatenate(rows, axis=0).astype(BF16)
     copies = [
         pltpu.make_async_copy(block_ref, out_hbm.at[i, pl.ds(0, FROWS + COMMON), :], sems.at[0]) for i in range(CHIPS)
     ]
@@ -89,9 +92,17 @@
         copy.start()
     zero = [jnp.zeros((1, DEVICES), F32)]
     turn_ref[...] = jnp.transpose(jnp.concatenate(own + zero * (DEVICES - len(own)), axis=0)) + ends.astype(F32)
-    spec_ref[...] = jnp.zeros((CHIPS * 8, 128), F32)
-    for c in range(2):
-        spec_ref[pl.ds(c, CHIPS, stride=8), :] = turn_ref[pl.ds(c, CHIPS, stride=2), :]
+    turned = turn_ref[...]
+    lanes = iota((DEVICES, 128), 1)
+    spec_ref[...] = jnp.broadcast_to(tail[None], (CHIPS, 8, 128)).reshape(CHIPS * 8, 128)
+    for j in range(2):
+        left = pltpu.roll(turned, (SPARE[0] - 2 * j * PIECE) % 128, 1)
+        right = pltpu.roll(turned, (SPARE[1] - (2 * j + 1) * PIECE) % 128, 1)
+        left = jnp.where((lanes >= SPARE[0]) & (lanes < SPARE[0] + PIECE), left, 0.0)
+        turn_ref[...] = left + jnp.where(lanes >= SPARE[1], right, 0.0)
+        for c in range(2):
+            at = pl.ds(2 * c + j, CHIPS, stride=8)
+            spec_ref[at, :] = spec_ref[at, :] + turn_ref[pl.ds(c, CHIPS, stride=2), :]
     send_ref[...] = spec_ref[...].astype(BF16).reshape(CHIPS, 8, 128)
     last = pltpu.make_async_copy(send_ref, out_hbm.at[:, pl.ds(FROWS + COMMON, 8), :], sems.at[1])
     last.start()
@@ -156,21 +167,26 @@
     d_f = d_lane.astype(F32)
     d_location = ((d_lane & 1) ^ core) * CHIPS + lax.shift_right_logical(d_lane, 1)
 
-    spec = jnp.concatenate(
-        [jnp.where(core == 0, field(k, COMMON), field(k, COMMON + 1)) for k in range(2)], axis=0
-    )
+    spec = jnp.zeros((DEVICES, DEVICES), F32)
+    for j in range(2):
+        row = [jnp.where(core == 0, field(k, COMMON + j), field(k, COMMON + 2 + j)) for k in range(2)]
+        row = jnp.concatenate(row, axis=0)
+        for e in range(2):
+            piece = 2 * j + e
+            back = pltpu.roll(row, (piece * PIECE - SPARE[e]) % 128, 1)
+            spec = jnp.where((d1 >= piece * PIECE) & (d1 < (piece + 1) * PIECE), back, spec)
     own = mm(spec, turn, TN)
 
     def mine(base):
         return own[base : base + CAP]
 
-    totals = jnp.broadcast_to(spec[:, 80:81], (DEVICES, DEVICES))
+    totals = jnp.broadcast_to(spec[:, ENDS + FRONT : ENDS + FRONT + 1], (DEVICES, DEVICES))
     offset = mm(flag(s_loc_lane < s_row), totals, NN) + half * s_f
     total = mm(flag(s_loc_lane == s_row), totals, NN) + half
     slot1 = full(0)
     parent1 = jnp.zeros((n, DEVICES), F32)
     for k in range(FRONT - 1):
-        ends = jnp.broadcast_to(spec[:, 64 + k : 65 + k], (DEVICES, DEVICES))
+        ends = jnp.broadcast_to(spec[:, ENDS + k : ENDS + k + 1], (DEVICES, DEVICES))
         parent1 = parent1 + jnp.where(jnp.concatenate([ends] * CAP, axis=0) <= slot1, 1.0, 0.0)
     slot = slot1 + half
     kept = (slot < total) & (offset + slot < KEPT)
@@ -309,7 +325,7 @@
                 for k in range(CHUNKS - 1):
                     wide = ranges_ref[half, i, k * FRONT : (k + 1) * FRONT].astype(F32)
                     front_ref[pl.ds(at + k, FRONT, stride=CHUNKS), :] = wide
-                tail = ranges_ref[half, i, FROWS - 8 : FROWS].astype(F32)
+                tail = table_ref[half, i, COMMON:].astype(F32)
                 front_ref[pl.ds(at + CHUNKS - 1, 8, stride=CHUNKS), :] = tail
                 front_ref[pl.ds(at + 9 * CHUNKS - 1, 8, stride=CHUNKS), :] = pltpu.roll(tail, 64, 1)
 
@@ -362,8 +378,7 @@
                 pair = [y_ref[u * 16 + v * 8 : u * 16 + v * 8 + 8, cut] * scales[2 * u + v] for v in range(2)]
                 x_ref[pl.ds(at, 16), cut] = jnp.concatenate(pair, axis=0).astype(BF16)
 
-    @pl.loop(0, SLOTS // UNROLL)
-    def _(i):
+    for i in range(SLOTS // UNROLL):
         form(0, i * UNROLL, x0_ref)
 
     xs, vs, stores = (x0_ref, x1_ref), (v0_ref, v1_ref), [None, None]

time: 99.4 us -> 97.4 us (0.980)
  waiting for transfers between devices: 13 us -> 11.4 us
    all_to_all x1, waiting for transfers between devices: 7.25 us -> 5.78 us  [on_device(): lax.all_to_all(block, OWNER[:3], split_axis=0, concat_axis=0, tiled=True)]
where the time goes in v4:
time: 97.4 us; the launch traced here: 96.7 us
  Pallas kernels  33.3 us (34%)
  local copies, waits for them, and re-layouts  29.2 us (30%)
  starting transfers between devices  15 us (15%)
  waiting for transfers between devices  11.4 us (12%)
  other arithmetic  7.62 us (8%)
    pallas_call x1, Pallas kernels, values(): pl.pallas_call(values_kernel, out_shape=jax.ShapeDtypeStruct((3, HANDS, S...  29.3 us
    all_to_all x1, starting transfers between devices, on_device(): lax.all_to_all(block, OWNER[:3], split_axis=0, concat_axis=0, tiled=True)  12 us
    reshape x1, local copies, waits for them, and re-layouts, on_device(): jnp.pad(policy_table, ((0, 1), (0, WIDTH - HANDS))).astype(F32)  11.8 us
    unnamed x5, local copies, waits for them, and re-layouts  9.9 us
    pad x1, other arithmetic, on_device(): policy = jnp.pad(policy, ((0, 13), (0, 0)))  7.62 us
    all_to_all x1, waiting for transfers between devices, on_device(): lax.all_to_all(block, OWNER[:3], split_axis=0, concat_axis=0, tiled=True)  5.78 us
    ppermute x1, waiting for transfers between devices, on_device(): other = lax.ppermute(mine, OWNER[3], [(0, 1), (1, 0)])  5.61 us
    pad x1, local copies, waits for them, and re-layouts, on_device(): weights_in = jnp.pad(value_in, ((0, WIDTH - HANDS), (0, 0)))  4.58 us
  transfers between devices with their start and end apart: 2, of which 2 were waited for; matrix products, arithmetic and copies ran while one was open for 36% of the time, Pallas kernels for 0%

profile of v4, /device:TPU:1, one launch (start us, length us, event | category | flops | bytes accessed | tf_op | source)
XLA Modules:
  0.0 96.7 jit_solution(11774071366717267496)
XLA Ops:
  0.0 4.0 %tables.1 = bf16[64,200,128]{2,1,0:T(8,128)(2,1)} custom-call(s32[16]{0:T(128)} %first_ref.1, s32[3,512]{1,0:T(4,128)} %owner_ref.1, s32[3,512]{1,0:T(4,128)} %policy_ref.1, s32[2,512]{1,0:T(2,128)} %next_ref.1, bf16[16,1326]{1,0:T(8,128)(2,1)} %frontier_ref.1), custom_call_target="tpu_custom_call" | custom-call | tf_op jit(solution)/shard_map/tables/pallas_call | solution.py:116
  4.0 12.0 %all-to-all-start = ((bf16[64,200,128]{2,1,0:T(8,128)(2,1)}), bf16[64,200,128]{2,1,0:T(8,128)(2,1)S(1)}, u32[]{:S(2)}, u32[]{:S(2)}) async-start(bf16[64,200,128]{2,1,0:T(8,128)(2,1)} %tables.1), calls=%async_computation | async-start | bytes 6553600 | tf_op jit(solution)/shard_map/all_to_all | solution.py:451
  16.0 8.2 %copy.10 = bf16[2048,1326]{1,0:T(8,128)(2,1)} copy(bf16[2048,1326]{0,1:T(8,128)(2,1)} %param.9) | data formatting | bytes 10862592
  24.1 0.0 copy-start
  24.1 4.6 %pad.18.in_hbm = bf16[1408,1536]{1,0:T(8,128)(2,1)} pad(bf16[1326,1536]{1,0:T(8,128)(2,1)} %param.14, bf16[]{:T(256)} %constant.8.clone.1), padding=0_82x0_0 | pad | bytes 8398850 | tf_op jit(solution)/shard_map/jit(_pad)/pad | solution.py:454
  28.7 0.0 copy-done
  28.8 2.9 %pad.15.clone = bf16[2049,1408]{1,0:T(8,128)(2,1)} pad(bf16[2048,1326]{1,0:T(8,128)(2,1)S(1)} %copy-done, bf16[]{:T(256)} %constant.8.clone.1), padding=0_1x0_82 | pad | bytes 11201282 | tf_op jit(solution)/shard_map/jit(_pad)/pad | solution.py:452
  31.7 11.8 %reshape.4 = bf16[22539,128]{1,0:T(8,128)(2,1)} reshape(bf16[2049,1408]{1,0:T(8,128)(2,1)} %pad.15.clone) | data formatting | bytes 11539968 | tf_op jit(solution)/shard_map/reshape | solution.py:452
  43.5 7.6 %pad_convert_fusion.policy_hbm = f32[22552,128]{1,0:T(8,128)} fusion(bf16[22539,128]{1,0:T(8,128)(2,1)} %reshape.4), kind=kLoop, calls=%fused_computation | loop fusion | flops 2886656 | bytes 17316608 | tf_op jit(solution)/shard_map/jit(_pad)/pad | solution.py:453
  51.1 5.8 %all-to-all-done.mine_ref = bf16[64,200,128]{2,1,0:T(8,128)(2,1)S(1)} async-done(((bf16[64,200,128]{2,1,0:T(8,128)(2,1)}), bf16[64,200,128]{2,1,0:T(8,128)(2,1)S(1)}, u32[]{:S(2)}, u32[]{:S(2)}) %all-to-all-start) | async-done | bytes 3276832 | tf_op jit(solution)/shard_map/all_to_all | solution.py:451
  56.9 0.0 copy-start.1
  56.9 1.7 %copy-done.1 = bf16[64,200,128]{2,1,0:T(8,128)(2,1)} copy-done((bf16[64,200,128]{2,1,0:T(8,128)(2,1)}, bf16[64,200,128]{2,1,0:T(8,128)(2,1)S(1)}, u32[]{:S(2)}) %copy-start.1) | copy-done | bytes 3276824
  58.6 3.0 %collective-permute-start = (bf16[64,200,128]{2,1,0:T(8,128)(2,1)S(1)}, bf16[64,200,128]{2,1,0:T(8,128)(2,1)}, u32[]{:S(2)}, u32[]{:S(2)}) collective-permute-start(bf16[64,200,128]{2,1,0:T(8,128)(2,1)S(1)} %all-to-all-done.mine_ref), channel_id=1, source_target_pairs={{0,1},{1,0},{2,3},{3,2},{4,5},{5,4},{6,7},{7,6},{8,9},{9,8},{10,11... | collective-permute-start | bytes 9830408 | tf_op jit(solution)/shard_map/ppermute | solution.py:456
  61.6 5.6 %collective-permute-done.other_ref = bf16[64,200,128]{2,1,0:T(8,128)(2,1)} collective-permute-done((bf16[64,200,128]{2,1,0:T(8,128)(2,1)S(1)}, bf16[64,200,128]{2,1,0:T(8,128)(2,1)}, u32[]{:S(2)}, u32[]{:S(2)}) %collective-permute-start) | collective-permute-done | bytes 3276832 | tf_op jit(solution)/shard_map/ppermute | solution.py:456
  67.2 29.3 %values.1 = bf16[3,1326,512]{2,1,0:T(8,128)(2,1)} custom-call(s32[1]{0:T(128)} %bitcast.core_ref, bf16[64,200,128]{2,1,0:T(8,128)(2,1)} %copy-done.1, bf16[64,200,128]{2,1,0:T(8,128)(2,1)} %collective-permute-done.other_ref, f32[22552,128]{1,0:T(8,128)} %pad_convert_fusion.policy_hbm, bf16[1408,1536]{1,0:T(8,128)(2,1)} %pad.18.in_hbm, bf16[1326,1536]{1,0:T(8,128)(2,1)} %bitcast.3), custom_call_target="tpu_custom_call" | custom-call | tf_op jit(solution)/shard_map/values/pallas_call | solution.py:417
Async XLA Ops:
  4.0 52.9 %all-to-all-start = ((bf16[64,200,128]{2,1,0:T(8,128)(2,1)}), bf16[64,200,128]{2,1,0:T(8,128)(2,1)S(1)}, u32[]{:S(2)}, u32[]{:S(2)}) async-start(bf16[64,200,128]{2,1,0:T(8,128)(2,1)} %tables.1), calls=%async_computation | async-start | bytes 6553600 | tf_op jit(solution)/shard_map/all_to_all | solution.py:451
  24.1 4.6 %copy-start = (bf16[2048,1326]{1,0:T(8,128)(2,1)S(1)}, bf16[2048,1326]{1,0:T(8,128)(2,1)}, u32[]{:S(2)}) copy-start(bf16[2048,1326]{1,0:T(8,128)(2,1)} %copy.10) | copy-start | bytes 16293892
  56.9 1.7 %copy-start.1 = (bf16[64,200,128]{2,1,0:T(8,128)(2,1)}, bf16[64,200,128]{2,1,0:T(8,128)(2,1)S(1)}, u32[]{:S(2)}) copy-start(bf16[64,200,128]{2,1,0:T(8,128)(2,1)S(1)} %all-to-all-done.mine_ref) | copy-start | bytes 9830404
  58.6 8.6 %collective-permute-start = (bf16[64,200,128]{2,1,0:T(8,128)(2,1)S(1)}, bf16[64,200,128]{2,1,0:T(8,128)(2,1)}, u32[]{:S(2)}, u32[]{:S(2)}) collective-permute-start(bf16[64,200,128]{2,1,0:T(8,128)(2,1)S(1)} %all-to-all-done.mine_ref), channel_id=1, source_target_pairs={{0,1},{1,0},{2,3},{3,2},{4,5},{5,4},{6,7},{7,6},{8,9},{9,8},{10,11... | collective-permute-start | bytes 9830408 | tf_op jit(solution)/shard_map/ppermute | solution.py:456
